TPU v7x, 32 devices: a whole 2x2x4 slice. The times are simulated.
32 devices in a mesh: gx: 2 (over core), gy: 4 (over y, x), gz: 4 (over z).
Axes of the slice: x: 2, y: 2, z: 4, core: 2. Of those that a mesh axis runs over, the one named last changes fastest.
Arguments:
- pressure_rhs: float32 [32, 128, 2048], P('gx', 'gy', 'gz'), may hold values from -6 to 6
- shift_diag: float32 [32, 128, 2048], P('gx', 'gy', 'gz'), may hold values from 0.02 to 0.3
- positions: float32 [3, 262144], P(None, ('gx', 'gy', 'gz')), may hold values from -6 to 6
- normals: float32 [3, 262144], P(None, ('gx', 'gy', 'gz')), may hold values from -6 to 6
- tension: float32 [262144], P(('gx', 'gy', 'gz')), may hold values from 0.3 to 3
- edge_weight: float32 [6, 262144], P(None, ('gx', 'gy', 'gz')), may hold values from 0.5 to 2
- owner_map: int32 [262144, 1], P(('gx', 'gy', 'gz')), may hold values from 0 to 31; in each aligned block of 8192 rows (0 to 8191, 8192 to 16383, ...) at most 1024 rows name the same one
- cell_map: int32 [262144], P(('gx', 'gy', 'gz')), may hold values from 0 to 262143
- connectivity: int32 [6, 262144], P(None, ('gx', 'gy', 'gz')), may hold values from 0 to 262143, as said below
Outputs:
- pressure: float32 [32, 128, 2048], P('gx', 'gy', 'gz')
- surface_force: float32 [3, 262144], P(None, ('gx', 'gy', 'gz'))
Inputs may be any that keep to these rules, and one draw needn't show every extreme that they name: `connectivity`: each neighbour index differs from the point's own index by 1 to 64, counted cyclically over 262144; the distance 64 occurs. `owner_map`: among the points of one device no owner is named more than 1024 times, a bound that some block reaches.
All inputs are finite; a program needn't handle non-finite values.
Results may differ from a plain program's by a relative error of at most 0.0003.
Values sent between devices are 32-bit elements; how exact they have to be, the bound alone decides.
A program may use at most 192 MiB of HBM per device.

v0:
```python
import jax
import jax.numpy as jnp
from jax import lax
from jax.sharding import PartitionSpec as P

HALO = 64
SMOOTH = 3
COARSE_SMOOTH = 4


centre = 1.125
spread = 0.875


def padded_2(cells, sides, width, closed):
    for axis, dim in sides:
        count = lax.axis_size(axis)
        ends = count if closed else count - 1
        head = lax.slice_in_dim(cells, 0, width, axis=dim)
        tail = lax.slice_in_dim(cells, cells.shape[dim] - width, cells.shape[dim], axis=dim)
        cells = jnp.concatenate(
            [
                lax.ppermute(tail, axis, [(i, (i + 1) % count) for i in range(ends)]),
                cells,
                lax.ppermute(head, axis, [((i + 1) % count, i) for i in range(ends)]),
            ],
            axis=dim,
        )
    return cells


def stencil(padded, field, shift):
    beside = padded[2:, 1:-1, 1:-1] + padded[:-2, 1:-1, 1:-1]
    beside = beside + padded[1:-1, 2:, 1:-1] + padded[1:-1, :-2, 1:-1]
    beside = beside + padded[1:-1, 1:-1, 2:] + padded[1:-1, 1:-1, :-2]
    return (6.0 + shift) * field - beside


def coarse_apply(field, shift):
    padded = padded_2(field, (("gx", 0), ("gy", 1), ("gz", 2)), 1, False)
    return stencil(padded, field, shift)


def local_apply(field, shift):
    return stencil(jnp.pad(field, 1), field, shift)


def chebyshev(target, shift, start, sweeps, apply_fn, inside):
    inverse = 1.0 / (6.0 + shift)
    ratio = centre / spread
    factor = 1.0 / ratio
    if start is None:
        update = inverse * target / centre
        answer = update
    else:
        update = inverse * (target - apply_fn(start, shift)) / centre
        update = update * inside
        answer = start + update
    for sweep in range(1, sweeps):
        remain = inverse * (target - apply_fn(answer, shift))
        if inside is not None:
            remain = remain * inside
        factor_new = 1.0 / (2.0 * ratio - factor)
        update = factor_new * factor * update + 2.0 * factor_new / spread * remain
        answer = answer + update
        factor = factor_new
    return answer


def domain_mask(shape, width):
    places = (lax.axis_index("gx"), lax.axis_index("gy"), lax.axis_index("gz"))
    counts = (lax.axis_size("gx"), lax.axis_size("gy"), lax.axis_size("gz"))
    factors = []
    for which in range(3):
        length = shape[which]
        where = places[which] * length - width + jnp.arange(length + 2 * width, dtype=jnp.int32)
        factors.append(((where >= 0) & (where < length * counts[which])).astype(jnp.float32))
    return factors[0][:, None, None] * factors[1][None, :, None] * factors[2][None, None, :]


def interior(field, width):
    return field[width:-width, width:-width, width:-width]


def blocks(field):
    return field.reshape(field.shape[0] // 2, 2, field.shape[1] // 2, 2, field.shape[2] // 2, 2)


def gather_neighbours(padded, relative, npoint):
    block_len = 2 * HALO
    nblock = npoint // block_len
    lower = padded[:, :npoint].reshape(3, nblock, block_len)
    upper = padded[:, block_len:].reshape(3, nblock, block_len)
    window = jnp.concatenate([lower, upper], axis=2)
    starts = (jnp.arange(nblock, dtype=jnp.int32) * block_len)[None, :, None]
    local_idx = relative.reshape(relative.shape[0], nblock, block_len) - starts
    columns = jnp.arange(2 * block_len, dtype=jnp.int32)
    picked = []
    for which in range(relative.shape[0]):
        select = (local_idx[which][:, :, None] == columns[None, None, :]).astype(jnp.float32)
        taken = jnp.einsum("bpw,cbw->cbp", select, window, precision=lax.Precision.HIGHEST)
        picked.append(taken.reshape(3, npoint))
    return jnp.stack(picked, axis=1)


def slot_ranks(owner_ids, ndevice, npoint):
    block_len = 2 * HALO
    nblock = npoint // block_len
    owner_hot = (owner_ids[:, None] == jnp.arange(ndevice, dtype=jnp.int32)[None, :]).astype(
        jnp.bfloat16
    )
    owner_blocks = owner_hot.reshape(nblock, block_len, ndevice)
    lower_tri = (jnp.arange(block_len)[:, None] > jnp.arange(block_len)[None, :]).astype(
        jnp.bfloat16
    )
    within = jnp.einsum("pq,bqo->bpo", lower_tri, owner_blocks, preferred_element_type=jnp.float32)
    counts = jnp.sum(owner_blocks.astype(jnp.float32), axis=1)
    before = jnp.cumsum(counts, axis=0) - counts
    ranks = jnp.sum((within + before[:, None, :]) * owner_blocks.astype(jnp.float32), axis=2)
    return (ranks.reshape(npoint).astype(jnp.int32), owner_hot)


def body(
    pressure_rhs,
    shift_diag,
    positions,
    normals,
    tension,
    edge_weight,
    owner_map,
    cell_map,
    connectivity,
):
    npoint = positions.shape[1]
    ndevice = lax.axis_size(("gx", "gy", "gz"))
    total = npoint * ndevice
    begin = lax.axis_index(("gx", "gy", "gz")) * npoint
    padded = padded_2(positions, ((("gx", "gy", "gz"), 1),), HALO, True)
    relative = (connectivity - begin + HALO + total) % total
    neighbours = gather_neighbours(padded, relative, npoint)
    surface_force = tension[None, :] * jnp.sum(
        edge_weight[None, :, :] * (neighbours - positions[:, None, :]), axis=1
    )
    jump = jnp.sum(surface_force * normals, axis=0)
    owner_ids = owner_map[:, 0]
    capacity = 4 * npoint // ndevice
    ranks, owner_hot = slot_ranks(owner_ids, ndevice, npoint)
    rank_hot = (ranks[:, None] == jnp.arange(capacity, dtype=jnp.int32)[None, :]).astype(
        jnp.float32
    )
    carried = jnp.stack([jump, cell_map.astype(jnp.float32)], axis=0)
    weighted = carried[:, :, None] * rank_hot[None, :, :]
    packed = jnp.einsum(
        "po,kpr->kor", owner_hot.astype(jnp.float32), weighted, precision=lax.Precision.HIGHEST
    )
    values = packed[0]
    cell_ids = packed[1]
    got_values, got_cells = (
        lax.all_to_all(values, ("gx", "gy", "gz"), split_axis=0, concat_axis=0, tiled=True),
        lax.all_to_all(cell_ids, ("gx", "gy", "gz"), split_axis=0, concat_axis=0, tiled=True),
    )
    shape = pressure_rhs.shape
    source = jnp.zeros((shape[0] * shape[1] * shape[2],), jnp.float32)
    source = source.at[got_cells.reshape(-1).astype(jnp.int32)].add(got_values.reshape(-1))
    forcing = pressure_rhs + source.reshape(shape)
    coarse_shift = 4.0 * jnp.mean(blocks(shift_diag), axis=(1, 3, 5))
    width = SMOOTH
    inside = domain_mask(shape, width)
    forcing_wide, shift_wide = (
        padded_2(forcing, (("gx", 0), ("gy", 1), ("gz", 2)), width, False),
        padded_2(shift_diag, (("gx", 0), ("gy", 1), ("gz", 2)), width, False),
    )
    smooth_wide = chebyshev(forcing_wide, shift_wide, None, SMOOTH, local_apply, inside)
    remain = interior(forcing_wide - local_apply(smooth_wide, shift_wide), width)
    smooth = interior(smooth_wide, width)
    coarse_rhs = 0.5 * jnp.sum(blocks(remain), axis=(1, 3, 5))
    coarse_fix = chebyshev(coarse_rhs, coarse_shift, None, COARSE_SMOOTH, coarse_apply, None)
    spreadout = jnp.broadcast_to(
        coarse_fix[:, None, :, None, :, None], blocks(shift_diag).shape
    ).reshape(shape)
    start_wide = padded_2(smooth + spreadout, (("gx", 0), ("gy", 1), ("gz", 2)), width, False)
    pressure = interior(
        chebyshev(forcing_wide, shift_wide, start_wide, SMOOTH, local_apply, inside), width
    )
    return (pressure, surface_force)


def solution(mesh):
    return jax.shard_map(
        body,
        mesh=mesh,
        in_specs=(
            P("gx", "gy", "gz"),
            P("gx", "gy", "gz"),
            P(None, ("gx", "gy", "gz")),
            P(None, ("gx", "gy", "gz")),
            P(("gx", "gy", "gz")),
            P(None, ("gx", "gy", "gz")),
            P(("gx", "gy", "gz"), None),
            P(("gx", "gy", "gz")),
            P(None, ("gx", "gy", "gz")),
        ),
        out_specs=(P("gx", "gy", "gz"), P(None, ("gx", "gy", "gz"))),
        check_vma=False,
    )
```

profile of v0, /device:TPU:0, one launch (start us, length us, event | category | flops | bytes accessed | tf_op | source)
XLA Modules:
  0.0 774.3 jit_solution(18078454126969736080)
XLA Ops:
  1.5 3.1 collective-permute-start.6
  4.5 3.4 collective-permute-start.7
  10.2 3.0 collective-permute-start
  16.1 11.2 %fusion.4 = f32[8192,1024]{1,0:T(8,128)} fusion(s32[8192]{0:T(1024)S(1)} %convert_bitcast_fusion), kind=kLoop, calls=%fused_computation.6 | loop fusion | flops 16777216 | bytes 33587200 | tf_op jit(solution)/shard_map/convert_element_type | solution.py:148
  27.6 4.3 fusion.10
  31.9 4.4 fusion.9
  36.3 4.4 fusion.8
  40.6 4.4 fusion.7
  45.0 4.4 fusion.6
  49.4 4.4 fusion.5
  54.9 30.9 %fusion.42 = f32[2,32,1024]{2,1,0:T(8,128)S(1)} fusion(f32[8192,1024]{1,0:T(8,128)} %fusion.4, f32[2,8192]{1,0:T(2,128)S(1)} %pad_maximum_fusion.81, s32[8192]{0:T(1024)S(1)} %bitcast.88), kind=kOutput, calls=%fused_computation.93 | convolution fusion | flops 6459490304 | bytes 33914880 | tf_op jit(solution)/shard_map/po,kpr->kor/dot_general | solution.py:153
  87.4 3.0 all-to-all-start
  90.5 7.8 %all-to-all-done = f32[32,1,1024]{2,1,0:T(1,128)S(1)} async-done(((f32[32,1,1024]{2,1,0:T(1,128)}), f32[32,1,1024]{2,1,0:T(1,128)S(1)}, u32[]{:S(2)}, u32[]{:S(2)}) %all-to-all-start) | async-done | bytes 131104 | tf_op jit(solution)/shard_map/all_to_all | solution.py:160
  98.3 2.6 all-to-all-start.1
  101.2 7.7 all-to-all-done.1
  108.9 219.4 %scatter_custom_fusion = f32[262144]{0:T(1024)S(1)} fusion(s32[32768]{0:T(1024)S(1)} %bitcast.91, f32[32768]{0:T(1024)S(1)} %bitcast.90, f32[]{:T(128)} %constant.30.clone.1), kind=kCustom, calls=%fused_computation.119 | custom fusion | flops 32768 | bytes 1048580 | tf_op jit(solution)/shard_map/scatter-add | solution.py:164
  329.4 1.7 add.306
  335.3 14.8 %collective-permute-start.2 = (f32[22,3,512]{2,1,0:T(4,128)}, f32[22,3,512]{2,1,0:T(4,128)S(1)}, u32[]{:S(2)}, u32[]{:S(2)}) collective-permute-start(f32[22,3,512]{2,1,0:T(4,128)} %get-tuple-element.33), channel_id=1, source_target_pairs={{0,4},{4,8},{8,12},{1,5},{5,9},{9,13},{2,6},{6,10},{10,14},{3,7},{... | collective-permute-start | bytes 405512 | tf_op jit(solution)/shard_map/ppermute | solution.py:23
  351.5 69.2 %reshape.186 = f32[8,2,16,2,256,2]{5,4,3,2,1,0:T(8,128)} reshape(f32[16,32,512]{2,1,0:T(8,128)} %param.10) | data formatting | bytes 2097152 | tf_op jit(solution)/shard_map/reshape | solution.py:86
  420.7 20.8 %reduce_sum.58 = f32[8,16,256]{2,1,0:T(8,128)S(1)} reduce(f32[8,2,16,2,256,2]{5,4,3,2,1,0:T(8,128)} %reshape.186, f32[]{:T(128)} %constant.30.clone.1), dimensions={1,3,5}, to_apply=%region_6.7 | reduce | flops 229376 | bytes 1179652 | tf_op jit(solution)/shard_map/reduce_sum | solution.py:166
  441.6 4.6 collective-permute-start.10
  447.7 2.9 collective-permute-start.4
  452.0 5.7 collective-permute-done.11
  459.2 1.4 collective-permute-start.13
  461.3 4.4 collective-permute-done.5
  465.7 3.5 broadcast_divide_fusion
  470.3 4.1 collective-permute-done.13
  475.6 2.7 multiply_add_fusion
  478.4 2.7 fusion.21
  481.1 1.9 slice_add_fusion
  483.0 3.0 fusion.48
  486.0 68.4 %reshape.187 = f32[8,2,16,2,256,2]{5,4,3,2,1,0:T(8,128)} reshape(f32[16,32,512]{2,1,0:T(8,128)S(1)} %fusion.48) | data formatting | bytes 2097152 | tf_op jit(solution)/shard_map/reshape | solution.py:86
  554.5 20.8 %reduce_sum.59 = f32[8,16,256]{2,1,0:T(8,128)S(1)} reduce(f32[8,2,16,2,256,2]{5,4,3,2,1,0:T(8,128)} %reshape.187, f32[]{:T(128)} %constant.30.clone.1), dimensions={1,3,5}, to_apply=%region_7.8 | reduce | flops 229376 | bytes 1179652 | tf_op jit(solution)/shard_map/reduce_sum | solution.py:176
  577.9 1.8 collective-permute-done.14
  579.7 4.3 collective-permute-start.17
  585.3 4.6 collective-permute-done.16
  591.4 4.6 collective-permute-start.19
  596.8 1.5 collective-permute-done.19
  601.2 1.8 collective-permute-done.20
  603.0 4.8 collective-permute-start.23
  609.2 4.2 collective-permute-done.22
  614.8 5.0 collective-permute-start.25
  620.7 1.5 collective-permute-done.25
  625.1 1.8 collective-permute-done.26
  626.9 2.8 collective-permute-start.29
  631.1 4.2 collective-permute-done.28
  635.4 1.5 collective-permute-start.30
  636.9 5.0 collective-permute-start.31
  642.8 1.5 collective-permute-done.31
  644.5 21.5 %broadcast_in_dim.5 = f32[8,2,16,2,256,2]{5,4,3,2,1,0:T(8,128)} broadcast(f32[8,16,256]{2,1,0:T(8,128)S(1)} %fusion.64), dimensions={0,2,4} | broadcast | bytes 1179648 | tf_op jit(solution)/shard_map/broadcast_in_dim | solution.py:178
  666.0 47.0 %reshape.188 = f32[16,32,512]{2,1,0:T(8,128)S(1)} reshape(f32[8,2,16,2,256,2]{5,4,3,2,1,0:T(8,128)} %broadcast_in_dim.5) | data formatting | bytes 2097152 | tf_op jit(solution)/shard_map/reshape | solution.py:180
  713.0 1.8 slice_add_fusion.6
  717.5 2.0 collective-permute-done.33
  719.6 2.8 collective-permute-start.34
  723.7 2.8 collective-permute-done.34
  726.5 4.6 collective-permute-done.35
  731.4 4.4 collective-permute-start.36
  735.7 1.4 collective-permute-start.37
  737.2 7.8 %collective-permute-done.36 = f32[22,38,3]{2,1,0:T(8,128)S(1)} collective-permute-done((f32[22,38,3]{2,1,0:T(8,128)S(1)}, f32[22,38,3]{2,1,0:T(8,128)S(1)}, u32[]{:S(2)}, u32[]{:S(2)}) %collective-permute-start.36) | collective-permute-done | bytes 10064 | tf_op jit(solution)/shard_map/ppermute | solution.py:23
  744.9 4.5 collective-permute-done.37
  750.6 2.6 fusion.100
  753.2 4.4 fusion.98
  757.6 9.2 %add_subtract_fusion = f32[22,38,518]{2,1,0:T(8,128)} fusion(f32[22,38,518]{2,1,0:T(8,128)} %get-tuple-element.4, f32[22,38,518]{2,1,0:T(8,128)S(1)} %get-tuple-element.3), kind=kLoop, calls=%fused_computation.45 | loop fusion | flops 3031336 | bytes 5196576 | tf_op jit(solution)/shard_map/sub | solution.py:36
  766.8 7.1 slice_add_fusion.1
  (135 shorter events, 46.8 us)
Async XLA Ops:
  0.6 15.2 %copy-start.14 = (s32[6,8192]{1,0:T(8,128)S(1)}, s32[6,8192]{1,0:T(8,128)}, u32[]{:S(2)}) copy-start(s32[6,8192]{1,0:T(8,128)} %param.17) | copy-start | bytes 589828
  1.5 25.9 %collective-permute-start.6 = (f32[3,64]{1,0:T(4,128)S(1)}, f32[3,64]{1,0:T(4,128)S(1)}, u32[]{:S(2)}, u32[]{:S(2)}) collective-permute-start(f32[3,64]{1,0:T(4,128)S(1)} %get-tuple-element.69), channel_id=1, source_target_pairs={{0,1},{1,2},{2,3},{3,4},{4,5},{5,6},{6,7},{7,8},{8,9},{9,10},{10,1... | collective-permute-start | bytes 2312 | tf_op jit(solution)/shard_map/ppermute | solution.py:23
  4.5 22.8 %collective-permute-start.7 = (f32[3,64]{1,0:T(4,128)S(1)}, f32[3,64]{1,0:T(4,128)S(1)}, u32[]{:S(2)}, u32[]{:S(2)}) collective-permute-start(f32[3,64]{1,0:T(4,128)S(1)} %get-tuple-element.70), channel_id=1, source_target_pairs={{1,0},{2,1},{3,2},{4,3},{5,4},{6,5},{7,6},{8,7},{9,8},{10,9},{11,1... | collective-permute-start | bytes 2312 | tf_op jit(solution)/shard_map/ppermute | solution.py:25
  8.9 81.6 %collective-permute-start.1 = (f32[3,32,512]{2,1,0:T(8,128)S(1)}, f32[3,32,512]{2,1,0:T(8,128)S(1)}, u32[]{:S(2)}, u32[]{:S(2)}) collective-permute-start(f32[3,32,512]{2,1,0:T(8,128)S(1)} %get-tuple-element.39), channel_id=1, source_target_pairs={{16,0},{17,1},{18,2},{19,3},{20,4},{21,5},{22,6},{23,7},{24,8},{25... | collective-permute-start | bytes 589832 | tf_op jit(solution)/shard_map/ppermute | solution.py:25
  10.2 80.2 %collective-permute-start = (f32[3,32,512]{2,1,0:T(8,128)S(1)}, f32[3,32,512]{2,1,0:T(8,128)S(1)}, u32[]{:S(2)}, u32[]{:S(2)}) collective-permute-start(f32[3,32,512]{2,1,0:T(8,128)S(1)} %get-tuple-element.40), channel_id=1, source_target_pairs={{0,16},{1,17},{2,18},{3,19},{4,20},{5,21},{6,22},{7,23},{8,24},{9,... | collective-permute-start | bytes 589832 | tf_op jit(solution)/shard_map/ppermute | solution.py:23
  16.1 11.2 %copy-start.18 = (s32[8192]{0:T(1024)S(1)}, s32[8192]{0:T(1024)}, u32[]{:S(2)}) copy-start(s32[8192]{0:T(1024)} %param.16) | copy-start | bytes 98308
  16.1 11.3 %copy-start.12 = (f32[3,8192]{1,0:T(4,128)S(1)}, f32[3,8192]{1,0:T(4,128)}, u32[]{:S(2)}) copy-start(f32[3,8192]{1,0:T(4,128)} %param.11) | copy-start | bytes 294916
  45.0 8.8 %copy-start.13 = (f32[6,8192]{1,0:T(8,128)S(1)}, f32[6,8192]{1,0:T(8,128)}, u32[]{:S(2)}) copy-start(f32[6,8192]{1,0:T(8,128)} %param.14) | copy-start | bytes 589828
  49.4 4.7 copy-start.16
  49.4 4.7 copy-start.17
  49.4 5.5 copy-start.15
  85.8 4.6 copy-start.5
  87.4 10.9 %all-to-all-start = ((f32[32,1,1024]{2,1,0:T(1,128)}), f32[32,1,1024]{2,1,0:T(1,128)S(1)}, u32[]{:S(2)}, u32[]{:S(2)}) async-start(f32[32,1,1024]{2,1,0:T(1,128)} %copy.11), calls=%async_computation | async-start | bytes 262144 | tf_op jit(solution)/shard_map/all_to_all | solution.py:160
  90.5 356.9 %copy-start.3 = (f32[22,32,512]{2,1,0:T(8,128)}, f32[22,32,512]{2,1,0:T(8,128)S(1)}, u32[]{:S(2)}) copy-start(f32[22,32,512]{2,1,0:T(8,128)S(1)} %constant_dynamic-update-slice_fusion) | copy-start | bytes 4325380
  98.3 10.6 %all-to-all-start.1 = ((f32[32,1,1024]{2,1,0:T(1,128)}), f32[32,1,1024]{2,1,0:T(1,128)S(1)}, u32[]{:S(2)}, u32[]{:S(2)}) async-start(f32[32,1,1024]{2,1,0:T(1,128)} %copy.12), calls=%async_computation.1 | async-start | bytes 262144 | tf_op jit(solution)/shard_map/all_to_all | solution.py:159
  331.9 109.5 %collective-permute-start.8 = (f32[3,32,512]{2,1,0:T(8,128)}, f32[3,32,512]{2,1,0:T(8,128)S(1)}, u32[]{:S(2)}, u32[]{:S(2)}) collective-permute-start(f32[3,32,512]{2,1,0:T(8,128)} %get-tuple-element.37), channel_id=1, source_target_pairs={{0,16},{1,17},{2,18},{3,19},{4,20},{5,21},{6,22},{7,23},{8,24},{9,... | collective-permute-start | bytes 589832 | tf_op jit(solution)/shard_map/ppermute | solution.py:23
  333.2 108.3 %collective-permute-start.9 = (f32[3,32,512]{2,1,0:T(8,128)}, f32[3,32,512]{2,1,0:T(8,128)S(1)}, u32[]{:S(2)}, u32[]{:S(2)}) collective-permute-start(f32[3,32,512]{2,1,0:T(8,128)} %get-tuple-element.38), channel_id=1, source_target_pairs={{16,0},{17,1},{18,2},{19,3},{20,4},{21,5},{22,6},{23,7},{24,8},{25... | collective-permute-start | bytes 589832 | tf_op jit(solution)/shard_map/ppermute | solution.py:25
  335.3 112.1 %collective-permute-start.2 = (f32[22,3,512]{2,1,0:T(4,128)}, f32[22,3,512]{2,1,0:T(4,128)S(1)}, u32[]{:S(2)}, u32[]{:S(2)}) collective-permute-start(f32[22,3,512]{2,1,0:T(4,128)} %get-tuple-element.33), channel_id=1, source_target_pairs={{0,4},{4,8},{8,12},{1,5},{5,9},{9,13},{2,6},{6,10},{10,14},{3,7},{... | collective-permute-start | bytes 405512 | tf_op jit(solution)/shard_map/ppermute | solution.py:23
  350.2 97.3 %collective-permute-start.3 = (f32[22,3,512]{2,1,0:T(4,128)}, f32[22,3,512]{2,1,0:T(4,128)S(1)}, u32[]{:S(2)}, u32[]{:S(2)}) collective-permute-start(f32[22,3,512]{2,1,0:T(4,128)} %get-tuple-element.34), channel_id=1, source_target_pairs={{4,0},{8,4},{12,8},{5,1},{9,5},{13,9},{6,2},{10,6},{14,10},{7,3},{... | collective-permute-start | bytes 405512 | tf_op jit(solution)/shard_map/ppermute | solution.py:25
  441.5 16.2 %copy-start.6 = (f32[3,32,512]{2,1,0:T(8,128)}, f32[3,32,512]{2,1,0:T(8,128)S(1)}, u32[]{:S(2)}) copy-start(f32[3,32,512]{2,1,0:T(8,128)S(1)} %collective-permute-done.8) | copy-start | bytes 589828
  441.5 16.1 %copy-start.8 = (f32[3,32,512]{2,1,0:T(8,128)}, f32[3,32,512]{2,1,0:T(8,128)S(1)}, u32[]{:S(2)}) copy-start(f32[3,32,512]{2,1,0:T(8,128)S(1)} %collective-permute-done.9) | copy-start | bytes 589828
  441.6 10.4 %collective-permute-start.10 = (f32[22,3,512]{2,1,0:T(4,128)S(1)}, f32[22,3,512]{2,1,0:T(4,128)S(1)}, u32[]{:S(2)}, u32[]{:S(2)}) collective-permute-start(f32[22,3,512]{2,1,0:T(4,128)S(1)} %get-tuple-element.31), channel_id=1, source_target_pairs={{0,4},{4,8},{8,12},{1,5},{5,9},{9,13},{2,6},{6,10},{10,14},{3,7},{... | collective-permute-start | bytes 405512 | tf_op jit(solution)/shard_map/ppermute | solution.py:23
  446.1 11.5 %collective-permute-start.11 = (f32[22,3,512]{2,1,0:T(4,128)S(1)}, f32[22,3,512]{2,1,0:T(4,128)S(1)}, u32[]{:S(2)}, u32[]{:S(2)}) collective-permute-start(f32[22,3,512]{2,1,0:T(4,128)S(1)} %get-tuple-element.32), channel_id=1, source_target_pairs={{4,0},{8,4},{12,8},{5,1},{9,5},{13,9},{6,2},{10,6},{14,10},{7,3},{... | collective-permute-start | bytes 405512 | tf_op jit(solution)/shard_map/ppermute | solution.py:25
  447.5 10.4 %copy-start.10 = (f32[22,3,512]{2,1,0:T(4,128)}, f32[22,3,512]{2,1,0:T(4,128)S(1)}, u32[]{:S(2)}) copy-start(f32[22,3,512]{2,1,0:T(4,128)S(1)} %collective-permute-done.2) | copy-start | bytes 405508
  447.5 10.4 %copy-start.11 = (f32[22,3,512]{2,1,0:T(4,128)}, f32[22,3,512]{2,1,0:T(4,128)S(1)}, u32[]{:S(2)}) copy-start(f32[22,3,512]{2,1,0:T(4,128)S(1)} %collective-permute-done.3) | copy-start | bytes 405508
  447.7 18.0 %copy-start.4 = (f32[22,32,512]{2,1,0:T(8,128)S(1)}, f32[22,32,512]{2,1,0:T(8,128)}, u32[]{:S(2)}) copy-start(f32[22,32,512]{2,1,0:T(8,128)} %copy-done.3) | copy-start | bytes 4325380
  447.7 13.6 %collective-permute-start.4 = (f32[22,38,3]{2,1,0:T(8,128)S(1)}, f32[22,38,3]{2,1,0:T(8,128)S(1)}, u32[]{:S(2)}, u32[]{:S(2)}) collective-permute-start(f32[22,38,3]{2,1,0:T(8,128)S(1)} %get-tuple-element.27), channel_id=1, source_target_pairs={{0,1},{1,2},{2,3},{4,5},{5,6},{6,7},{8,9},{9,10},{10,11},{12,13},{... | collective-permute-start | bytes 30104 | tf_op jit(solution)/shard_map/ppermute | solution.py:23
  450.6 15.1 %collective-permute-start.5 = (f32[22,38,3]{2,1,0:T(8,128)S(1)}, f32[22,38,3]{2,1,0:T(8,128)S(1)}, u32[]{:S(2)}, u32[]{:S(2)}) collective-permute-start(f32[22,38,3]{2,1,0:T(8,128)S(1)} %get-tuple-element.28), channel_id=1, source_target_pairs={{1,0},{2,1},{3,2},{5,4},{6,5},{7,6},{9,8},{10,9},{11,10},{13,12},{... | collective-permute-start | bytes 30104 | tf_op jit(solution)/shard_map/ppermute | solution.py:25
  457.9 12.4 %collective-permute-start.12 = (f32[22,38,3]{2,1,0:T(8,128)S(1)}, f32[22,38,3]{2,1,0:T(8,128)S(1)}, u32[]{:S(2)}, u32[]{:S(2)}) collective-permute-start(f32[22,38,3]{2,1,0:T(8,128)S(1)} %get-tuple-element.25), channel_id=1, source_target_pairs={{0,1},{1,2},{2,3},{4,5},{5,6},{6,7},{8,9},{9,10},{10,11},{12,13},{... | collective-permute-start | bytes 30104 | tf_op jit(solution)/shard_map/ppermute | solution.py:23
  459.2 15.2 %copy-start.7 = (f32[3,32,512]{2,1,0:T(8,128)S(1)}, f32[3,32,512]{2,1,0:T(8,128)}, u32[]{:S(2)}) copy-start(f32[3,32,512]{2,1,0:T(8,128)} %copy-done.6) | copy-start | bytes 589828
  459.2 15.2 %copy-start.9 = (f32[3,32,512]{2,1,0:T(8,128)S(1)}, f32[3,32,512]{2,1,0:T(8,128)}, u32[]{:S(2)}) copy-start(f32[3,32,512]{2,1,0:T(8,128)} %copy-done.8) | copy-start | bytes 589828
  459.2 15.2 %collective-permute-start.13 = (f32[22,38,3]{2,1,0:T(8,128)S(1)}, f32[22,38,3]{2,1,0:T(8,128)S(1)}, u32[]{:S(2)}, u32[]{:S(2)}) collective-permute-start(f32[22,38,3]{2,1,0:T(8,128)S(1)} %get-tuple-element.26), channel_id=1, source_target_pairs={{1,0},{2,1},{3,2},{5,4},{6,5},{7,6},{9,8},{10,9},{11,10},{13,12},{... | collective-permute-start | bytes 30104 | tf_op jit(solution)/shard_map/ppermute | solution.py:25
  475.6 7.4 copy-start
  481.1 1.9 copy-start.2
  575.3 2.6 collective-permute-start.15
  576.6 3.1 collective-permute-start.14
  579.7 5.6 collective-permute-start.17
  584.0 5.9 collective-permute-start.16
  590.1 6.8 collective-permute-start.18
  591.4 7.0 collective-permute-start.19
  598.6 2.6 collective-permute-start.21
  599.9 3.1 collective-permute-start.20
  603.0 6.2 collective-permute-start.23
  607.8 5.6 collective-permute-start.22
  613.5 7.2 collective-permute-start.24
  614.8 7.4 collective-permute-start.25
  622.5 2.6 collective-permute-start.27
  623.8 3.1 collective-permute-start.26
  626.9 4.2 collective-permute-start.29
  629.7 5.6 collective-permute-start.28
  635.4 7.4 collective-permute-start.30
  636.9 7.4 collective-permute-start.31
  714.9 2.6 collective-permute-start.32
  716.2 3.3 collective-permute-start.33
  719.6 6.9 collective-permute-start.34
  722.4 8.7 %collective-permute-start.35 = (f32[22,3,512]{2,1,0:T(4,128)S(1)}, f32[22,3,512]{2,1,0:T(4,128)S(1)}, u32[]{:S(2)}, u32[]{:S(2)}) collective-permute-start(f32[22,3,512]{2,1,0:T(4,128)S(1)} %get-tuple-element.30), channel_id=1, source_target_pairs={{4,0},{8,4},{12,8},{5,1},{9,5},{13,9},{6,2},{10,6},{14,10},{7,3},{... | collective-permute-start | bytes 405512 | tf_op jit(solution)/shard_map/ppermute | solution.py:25
  731.4 13.6 %collective-permute-start.36 = (f32[22,38,3]{2,1,0:T(8,128)S(1)}, f32[22,38,3]{2,1,0:T(8,128)S(1)}, u32[]{:S(2)}, u32[]{:S(2)}) collective-permute-start(f32[22,38,3]{2,1,0:T(8,128)S(1)} %get-tuple-element.23), channel_id=1, source_target_pairs={{0,1},{1,2},{2,3},{4,5},{5,6},{6,7},{8,9},{9,10},{10,11},{12,13},{... | collective-permute-start | bytes 30104 | tf_op jit(solution)/shard_map/ppermute | solution.py:23
  735.7 14.9 %copy-start.1 = (f32[22,38,518]{2,1,0:T(8,128)S(1)}, f32[22,38,518]{2,1,0:T(8,128)}, u32[]{:S(2)}) copy-start(f32[22,38,518]{2,1,0:T(8,128)} %copy-done) | copy-start | bytes 5196580
  735.7 13.7 %collective-permute-start.37 = (f32[22,38,3]{2,1,0:T(8,128)S(1)}, f32[22,38,3]{2,1,0:T(8,128)S(1)}, u32[]{:S(2)}, u32[]{:S(2)}) collective-permute-start(f32[22,38,3]{2,1,0:T(8,128)S(1)} %get-tuple-element.24), channel_id=1, source_target_pairs={{1,0},{2,1},{3,2},{5,4},{6,5},{7,6},{9,8},{10,9},{11,10},{13,12},{... | collective-permute-start | bytes 30104 | tf_op jit(solution)/shard_map/ppermute | solution.py:25
where the time goes:
time: 780 us; the launch traced here: 774 us
  other arithmetic  320 us (41%)
  local copies, waits for them, and re-layouts  213 us (27%)
  starting transfers between devices  102 us (13%)
  waiting for transfers between devices  78.9 us (10%)
  matrix products  58.4 us (7%)
    scatter-add x1, other arithmetic, body(): source.at[got_cells.reshape(-1).astype(jnp.int32)]  219 us
    reshape x2, local copies, waits for them, and re-layouts, blocks(): field.reshape(field.shape[0] // 2, 2, field.shape[1] // 2, 2, field.shape...  138 us
    ppermute x19, starting transfers between devices, padded_2(): lax.ppermute(tail, axis, [(i, (i + 1) % count) for i in range(ends)])  69.8 us
    reshape x1, local copies, waits for them, and re-layouts, body(): spreadout = jnp.broadcast_to(coarse_fix[:, None, :, None, :, None], block...  47 us
    ppermute x19, waiting for transfers between devices, padded_2(): lax.ppermute(head, axis, [((i + 1) % count, i) for i in range(ends)])  46.4 us
    dot_general x1, matrix products, body(): jnp.einsum('po,kpr->kor', owner_hot.astype(jnp.float32), weighted, precis...  30.9 us
    ppermute x19, starting transfers between devices, padded_2(): lax.ppermute(head, axis, [((i + 1) % count, i) for i in range(ends)])  27.1 us
    dot_general x6, matrix products, gather_neighbours(): jnp.einsum('bpw,cbw->cbp', select, window, precision=lax.Precision.HIGHEST)  26.2 us
  transfers between devices with their start and end apart: 40, of which 27 were waited for; matrix products, arithmetic and copies ran while one was open for 22% of the time, Pallas kernels for 0%

commit v1 on v0

v1 whole, which is shorter than its diff:
```python
import functools

import jax
import jax.numpy as jnp
from jax import lax
from jax.experimental import pallas as pl
from jax.experimental.pallas import tpu as pltpu
from jax.sharding import PartitionSpec as P

HALO = 64
SMOOTH = 3
COARSE_SMOOTH = 4


centre = 1.125
spread = 0.875


def padded_2(cells, sides, width, closed):
    for axis, dim in sides:
        count = lax.axis_size(axis)
        ends = count if closed else count - 1
        head = lax.slice_in_dim(cells, 0, width, axis=dim)
        tail = lax.slice_in_dim(cells, cells.shape[dim] - width, cells.shape[dim], axis=dim)
        cells = jnp.concatenate(
            [
                lax.ppermute(tail, axis, [(i, (i + 1) % count) for i in range(ends)]),
                cells,
                lax.ppermute(head, axis, [((i + 1) % count, i) for i in range(ends)]),
            ],
            axis=dim,
        )
    return cells


def stencil(padded, field, shift):
    beside = padded[2:, 1:-1, 1:-1] + padded[:-2, 1:-1, 1:-1]
    beside = beside + padded[1:-1, 2:, 1:-1] + padded[1:-1, :-2, 1:-1]
    beside = beside + padded[1:-1, 1:-1, 2:] + padded[1:-1, 1:-1, :-2]
    return (6.0 + shift) * field - beside


def local_apply(field, shift):
    return stencil(jnp.pad(field, 1), field, shift)


def chebyshev(target, shift, start, sweeps, apply_fn, inside):
    inverse = 1.0 / (6.0 + shift)
    ratio = centre / spread
    factor = 1.0 / ratio
    if start is None:
        update = inverse * target / centre
        answer = update
    else:
        update = inverse * (target - apply_fn(start, shift)) / centre
        update = update * inside
        answer = start + update
    for sweep in range(1, sweeps):
        remain = inverse * (target - apply_fn(answer, shift))
        if inside is not None:
            remain = remain * inside
        factor_new = 1.0 / (2.0 * ratio - factor)
        update = factor_new * factor * update + 2.0 * factor_new / spread * remain
        answer = answer + update
        factor = factor_new
    return answer


def domain_mask(shape, width):
    places = (lax.axis_index("gx"), lax.axis_index("gy"), lax.axis_index("gz"))
    counts = (lax.axis_size("gx"), lax.axis_size("gy"), lax.axis_size("gz"))
    factors = []
    for which in range(3):
        length = shape[which]
        where = places[which] * length - width + jnp.arange(length + 2 * width, dtype=jnp.int32)
        factors.append(((where >= 0) & (where < length * counts[which])).astype(jnp.float32))
    return factors[0][:, None, None] * factors[1][None, :, None] * factors[2][None, None, :]


def interior(field, width):
    return field[width:-width, width:-width, width:-width]


LANES = 2 * HALO
HIGH = lax.Precision.HIGHEST


def pair_matrix(rows, cols, offset=0):
    r = lax.broadcasted_iota(jnp.int32, (rows, cols), 0)
    c = lax.broadcasted_iota(jnp.int32, (rows, cols), 1)
    return (r == (c + offset) // 2).astype(jnp.float32)


def pool(field):
    nx, ny, nz = field.shape
    halves = jnp.sum(field.reshape(nx // 2, 2, ny, nz), axis=1)
    flat = halves.reshape(nx // 2 * ny, nz)
    along_z = jnp.dot(flat, pair_matrix(nz // 2, nz).T, precision=HIGH)
    along_y = jnp.dot(
        pair_matrix(nx // 2 * ny // 2, nx // 2 * ny), along_z, precision=HIGH
    )
    return along_y.reshape(nx // 2, ny // 2, nz // 2)


def spread_out(coarse, crop):
    nx, ny, nz = coarse.shape
    along_z = jnp.dot(
        coarse.reshape(nx * ny, nz), pair_matrix(nz, 2 * nz - 2 * crop, crop), precision=HIGH
    ).reshape(nx, ny, 2 * nz - 2 * crop)
    fan = jnp.broadcast_to(
        pair_matrix(ny, 2 * ny - 2 * crop, crop).T[None], (nx, 2 * ny - 2 * crop, ny)
    )
    along_y = jnp.einsum("xyb,xbc->xyc", fan, along_z, precision=HIGH)
    twice = jnp.broadcast_to(along_y[:, None], (nx, 2) + along_y.shape[1:])
    twice = twice.reshape((2 * nx,) + along_y.shape[1:])
    return twice[crop : 2 * nx - crop]


def split3(x):
    a = x.astype(jnp.bfloat16)
    rest = x - a.astype(jnp.float32)
    b = rest.astype(jnp.bfloat16)
    c = (rest - b.astype(jnp.float32)).astype(jnp.bfloat16)
    return a, b, c


def points_kernel(
    ndevice, capacity, pos_ref, nrm_ref, ten_ref, wgt_ref, con_ref, own_ref, cel_ref,
    force_ref, packed_ref, carry_ref,
):
    step = pl.program_id(0)
    chunk = ten_ref.shape[1]

    @pl.when(step == 0)
    def _():
        packed_ref[...] = jnp.zeros_like(packed_ref)
        carry_ref[...] = jnp.zeros_like(carry_ref)

    jumps = []
    for sub in range(chunk // LANES):
        here = pl.ds(sub * LANES, LANES)
        base = pl.multiple_of(step * chunk + sub * LANES, LANES)
        lower = pos_ref[:, pl.ds(base, LANES)]
        upper = pos_ref[:, pl.ds(base + LANES, LANES)]
        centre_pos = jnp.concatenate([lower[:, HALO:], upper[:, :HALO]], axis=1)
        total = jnp.zeros_like(lower)
        for which in range(con_ref.shape[0]):
            index = con_ref[which : which + 1, here] - base
            wide = jnp.broadcast_to(index, lower.shape)
            low = jnp.bitwise_and(wide, LANES - 1)
            near = jnp.take_along_axis(lower, low, axis=1, mode="promise_in_bounds")
            far = jnp.take_along_axis(upper, low, axis=1, mode="promise_in_bounds")
            picked = jnp.where(wide < LANES, near, far)
            total = total + wgt_ref[which : which + 1, here] * (picked - centre_pos)
        force = ten_ref[:, here] * total[:3]
        force_ref[:, here] = force
        jumps.append(jnp.sum(force * nrm_ref[:, here], axis=0, keepdims=True))
    jump = jnp.concatenate(jumps, axis=1)

    hot = (lax.broadcasted_iota(jnp.int32, (ndevice, chunk), 0) == own_ref[...]).astype(jnp.float32)
    hot_half = hot.astype(jnp.bfloat16)
    before = (
        lax.broadcasted_iota(jnp.int32, (chunk, chunk), 0)
        < lax.broadcasted_iota(jnp.int32, (chunk, chunk), 1)
    ).astype(jnp.bfloat16)
    earlier = jnp.dot(hot_half, before, preferred_element_type=jnp.float32) + carry_ref[...]
    rank = jnp.sum(hot * earlier, axis=0, keepdims=True).astype(jnp.int32)
    carry_ref[...] = carry_ref[...] + jnp.sum(hot, axis=1, keepdims=True)
    slots = (
        lax.broadcasted_iota(jnp.int32, (capacity, chunk), 0) == rank
    ).astype(jnp.float32).astype(jnp.bfloat16)
    cell = cel_ref[...]
    parts = [piece.astype(jnp.float32) for piece in split3(jump)]
    for bits in (0, 8, 16):
        piece = jnp.bitwise_and(jnp.right_shift(cell, bits), 255).astype(jnp.float32)
        parts.append(piece)
    left = jnp.concatenate([(hot * part).astype(jnp.bfloat16) for part in parts], axis=0)
    packed = lax.dot_general(
        left, slots, (((1,), (1,)), ((), ())), preferred_element_type=jnp.float32
    )
    n = ndevice
    values = packed[0:n] + packed[n : 2 * n] + packed[2 * n : 3 * n]
    cells = packed[3 * n : 4 * n] + 256.0 * packed[4 * n : 5 * n] + 65536.0 * packed[5 * n :]
    packed_ref[:, :capacity] += values
    packed_ref[:, capacity:] += cells


def points(padded, normals, tension, edge_weight, relative, owner_ids, cell_map, ndevice, capacity):
    npoint = tension.shape[0]
    chunk = 4 * LANES if npoint % (4 * LANES) == 0 else LANES
    padded = jnp.concatenate([padded, jnp.zeros((5, padded.shape[1]), jnp.float32)], axis=0)
    neigh = relative.shape[0]

    def rows(count):
        return pl.BlockSpec((count, chunk), lambda i: (0, i))

    return pl.pallas_call(
        functools.partial(points_kernel, ndevice, capacity),
        grid=(npoint // chunk,),
        in_specs=[
            pl.BlockSpec(padded.shape, lambda i: (0, 0)),
            rows(3), rows(1), rows(neigh), rows(neigh), rows(1), rows(1),
        ],
        out_specs=[rows(3), pl.BlockSpec((ndevice, 2 * capacity), lambda i: (0, 0))],
        out_shape=[
            jax.ShapeDtypeStruct((3, npoint), jnp.float32),
            jax.ShapeDtypeStruct((ndevice, 2 * capacity), jnp.float32),
        ],
        scratch_shapes=[pltpu.VMEM((ndevice, 1), jnp.float32)],
        cost_estimate=pl.CostEstimate(
            flops=2 * npoint * capacity * 6 * ndevice, bytes_accessed=40000000, transcendentals=0
        ),
    )(
        padded, normals, tension[None], edge_weight, relative, owner_ids[None], cell_map[None]
    )


def scatter_kernel(rhs_ref, val_ref, row_ref, col_ref, out_ref):
    @pl.when(pl.program_id(0) == 0)
    def _():
        out_ref[...] = rhs_ref[...]

    nrow, ncol = out_ref.shape
    count = val_ref.shape[2]
    value = val_ref[0]
    first = value.astype(jnp.bfloat16)
    second = (value - first.astype(jnp.float32)).astype(jnp.bfloat16)
    by_row = (
        (lax.broadcasted_iota(jnp.int32, (nrow, count), 0) == row_ref[0])
        .astype(jnp.float32)
        .astype(jnp.bfloat16)
    )
    same = lax.broadcasted_iota(jnp.int32, (ncol, count), 0) == col_ref[0]
    total = out_ref[...]
    for piece in (first, second):
        by_col = jnp.where(same, piece.astype(jnp.float32), 0.0).astype(jnp.bfloat16)
        total = total + lax.dot_general(
            by_row, by_col, (((1,), (1,)), ((), ())), preferred_element_type=jnp.float32
        )
    out_ref[...] = total


def scatter(rhs, values, cells):
    nx, ny, nz = rhs.shape
    nrow = nx * ny
    sources, count = values.shape
    rows = cells // nz
    cols = cells - rows * nz
    one = pl.BlockSpec((1, 1, count), lambda i: (i, 0, 0))
    whole = pl.BlockSpec((nrow, nz), lambda i: (0, 0))
    out = pl.pallas_call(
        scatter_kernel,
        grid=(sources,),
        in_specs=[whole, one, one, one],
        out_specs=whole,
        out_shape=jax.ShapeDtypeStruct((nrow, nz), jnp.float32),
        cost_estimate=pl.CostEstimate(
            flops=4 * nrow * nz * sources * count, bytes_accessed=4000000, transcendentals=0
        ),
    )(rhs.reshape(nrow, nz), values[:, None], rows[:, None], cols[:, None])
    return out.reshape(nx, ny, nz)


def body(
    pressure_rhs,
    shift_diag,
    positions,
    normals,
    tension,
    edge_weight,
    owner_map,
    cell_map,
    connectivity,
):
    npoint = positions.shape[1]
    ndevice = lax.axis_size(("gx", "gy", "gz"))
    total = npoint * ndevice
    begin = lax.axis_index(("gx", "gy", "gz")) * npoint
    padded = padded_2(positions, ((("gx", "gy", "gz"), 1),), HALO, True)
    relative = (connectivity - begin + HALO + total) % total
    capacity = 4 * npoint // ndevice
    surface_force, packed = points(
        padded, normals, tension, edge_weight, relative, owner_map[:, 0], cell_map,
        ndevice, capacity,
    )
    got = lax.all_to_all(packed, ("gx", "gy", "gz"), split_axis=0, concat_axis=0, tiled=True)
    forcing = scatter(pressure_rhs, got[:, :capacity], got[:, capacity:].astype(jnp.int32))

    sides = (("gx", 0), ("gy", 1), ("gz", 2))
    shape = pressure_rhs.shape
    coarse_shift = 0.5 * pool(shift_diag)
    last = SMOOTH
    width = SMOOTH + SMOOTH - 1
    reach = (last + 1) // 2
    coarse_width = COARSE_SMOOTH - 1 + reach
    shift_wide = padded_2(shift_diag, sides, width, False)
    forcing_wide = padded_2(forcing, sides, width, False)
    smooth_wide = chebyshev(
        forcing_wide, shift_wide, None, SMOOTH, local_apply, domain_mask(shape, width)
    )
    near = slice(width - 1, -(width - 1))
    near = (near, near, near)
    remain = interior(forcing_wide, width) - stencil(
        smooth_wide[near], interior(smooth_wide, width), interior(shift_wide, width)
    )
    coarse_rhs = 0.5 * pool(remain)
    coarse_sides = (("gx", 1), ("gy", 2), ("gz", 3))
    coarse_wide = padded_2(
        jnp.stack([coarse_rhs, coarse_shift]), coarse_sides, coarse_width, False
    )
    coarse_fix = chebyshev(
        coarse_wide[0], coarse_wide[1], None, COARSE_SMOOTH, local_apply,
        domain_mask(coarse_rhs.shape, coarse_width),
    )
    coarse_fix = interior(coarse_fix, coarse_width - reach)
    spreadout = spread_out(coarse_fix, 2 * reach - last)
    trim = width - last
    start_wide = interior(smooth_wide, trim) + spreadout
    pressure = interior(
        chebyshev(
            interior(forcing_wide, trim), interior(shift_wide, trim), start_wide, SMOOTH,
            local_apply, domain_mask(shape, last),
        ),
        last,
    )
    return (pressure, surface_force)


def solution(mesh):
    return jax.shard_map(
        body,
        mesh=mesh,
        in_specs=(
            P("gx", "gy", "gz"),
            P("gx", "gy", "gz"),
            P(None, ("gx", "gy", "gz")),
            P(None, ("gx", "gy", "gz")),
            P(("gx", "gy", "gz")),
            P(None, ("gx", "gy", "gz")),
            P(("gx", "gy", "gz"), None),
            P(("gx", "gy", "gz")),
            P(None, ("gx", "gy", "gz")),
        ),
        out_specs=(P("gx", "gy", "gz"), P(None, ("gx", "gy", "gz"))),
        check_vma=False,
    )
```

time: 780 us -> 332 us (0.43)
  other arithmetic: 320 us -> 73.7 us
  local copies, waits for them, and re-layouts: 213 us -> 97.7 us
  Pallas kernels: 0 us -> 61.5 us
  waiting for transfers between devices: 78.9 us -> 22.4 us
  matrix products: 58.4 us -> 4.81 us
  starting transfers between devices: 102 us -> 65.9 us
    scatter-add x1 -> x0, other arithmetic: 219 us -> none  [body(): source.at[got_cells.reshape(-1).astype(jnp.int32)]]
    reshape x4 -> x0, local copies, waits for them, and re-layouts: 186 us -> none  [the longest x2 138 us: blocks(): field.reshape(field.shape[0] // 2, 2, field.shape[1] // 2, 2, field.shape...]
    pallas_call x0 -> x2, Pallas kernels: none -> 61.5 us  [the longest x1 46.5 us: scatter(): pl.pallas_call(scatter_kernel, grid=(sources,), in_specs=[whole, one, one...]
    dot_general x8 -> x6, matrix products: 58.4 us -> 4.81 us  [the longest x1 1.44 us: spread_out(): jnp.dot(coarse.reshape(nx * ny, nz), pair_matrix(nz, 2 * nz - 2 * crop, c...]
    reduce_sum x5 -> x1, other arithmetic: 43.6 us -> 2.03 us  [pool(): halves = jnp.sum(field.reshape(nx // 2, 2, ny, nz), axis=1)]
    ppermute x0 -> x10, local copies, waits for them, and re-layouts: none -> 39.9 us  [the longest x5 20.4 us: padded_2(): lax.ppermute(tail, axis, [(i, (i + 1) % count) for i in range(ends)])]
    ppermute x19 -> x10, starting transfers between devices: 69.8 us -> 35.1 us  [padded_2(): lax.ppermute(tail, axis, [(i, (i + 1) % count) for i in range(ends)])]
    ppermute x19 -> x10, waiting for transfers between devices: 46.4 us -> 14.6 us  [padded_2(): lax.ppermute(head, axis, [((i + 1) % count, i) for i in range(ends)])]
  transfers between devices with their start and end apart: 40 -> 21, of which waited for: 27 -> 5; matrix products, arithmetic and copies ran while one was open for 22% -> 32% of each run, Pallas kernels for 0% -> 19%
where the time goes in v1:
time: 332 us; the launch traced here: 328 us
  local copies, waits for them, and re-layouts  97.7 us (29%)
  other arithmetic  73.7 us (22%)
  starting transfers between devices  65.9 us (20%)
  Pallas kernels  61.5 us (19%)
  waiting for transfers between devices  22.4 us (7%)
  matrix products  4.81 us (1%)
    pallas_call x1, Pallas kernels, scatter(): pl.pallas_call(scatter_kernel, grid=(sources,), in_specs=[whole, one, one...  46.5 us
    ppermute x10, starting transfers between devices, padded_2(): lax.ppermute(tail, axis, [(i, (i + 1) % count) for i in range(ends)])  35.1 us
    concatenate x6, local copies, waits for them, and re-layouts, padded_2(): jnp.concatenate([lax.ppermute(tail, axis, [(i, (i + 1) % count) for i in...  31.6 us
    add x6, other arithmetic, chebyshev(): answer = answer + update  29 us
    ppermute x10, starting transfers between devices, padded_2(): lax.ppermute(head, axis, [((i + 1) % count, i) for i in range(ends)])  27.7 us
    concatenate x6, other arithmetic, padded_2(): jnp.concatenate([lax.ppermute(tail, axis, [(i, (i + 1) % count) for i in...  25 us
    ppermute x5, local copies, waits for them, and re-layouts, padded_2(): lax.ppermute(tail, axis, [(i, (i + 1) % count) for i in range(ends)])  20.4 us
    ppermute x5, local copies, waits for them, and re-layouts, padded_2(): lax.ppermute(head, axis, [((i + 1) % count, i) for i in range(ends)])  19.5 us
  transfers between devices with their start and end apart: 21, of which 5 were waited for; matrix products, arithmetic and copies ran while one was open for 32% of the time, Pallas kernels for 19%

profile of v1, /device:TPU:0, one launch (start us, length us, event | category | flops | bytes accessed | tf_op | source)
XLA Modules:
  0.0 328.0 jit_solution(6013128087261401833)
XLA Ops:
  1.4 3.1 collective-permute-start.6
  4.5 3.4 %collective-permute-start.7 = (f32[3,64]{1,0:T(4,128)S(1)}, f32[3,64]{1,0:T(4,128)S(1)}, u32[]{:S(2)}, u32[]{:S(2)}) collective-permute-start(f32[3,64]{1,0:T(4,128)S(1)} %get-tuple-element.49), channel_id=1, source_target_pairs={{1,0},{2,1},{3,2},{4,3},{5,4},{6,5},{7,6},{8,7},{9,8},{10,9},{11,1... | collective-permute-start | bytes 2312 | tf_op jit(solution)/shard_map/ppermute | solution.py:29
  9.0 3.3 %collective-permute-start = (f32[5,32,512]{2,1,0:T(8,128)S(1)}, f32[5,32,512]{2,1,0:T(8,128)}, u32[]{:S(2)}, u32[]{:S(2)}) collective-permute-start(f32[5,32,512]{2,1,0:T(8,128)S(1)} %get-tuple-element.42), channel_id=1, source_target_pairs={{0,16},{1,17},{2,18},{3,19},{4,20},{5,21},{6,22},{7,23},{8,24},{9,... | collective-permute-start | bytes 983048 | tf_op jit(solution)/shard_map/ppermute | solution.py:27
  12.3 1.3 collective-permute-start.1
  14.8 1.8 add_select_fusion.con_ref
  19.1 15.0 %shard_map.104 = (f32[3,8192]{1,0:T(4,128)}, f32[32,2048]{1,0:T(8,128)}) custom-call(f32[8,8320]{1,0:T(8,128)} %concatenate.37.pos_ref, f32[3,8192]{1,0:T(4,128)} %nrm_ref.1, f32[1,8192]{1,0:T(1,128)} %bitcast.83, f32[6,8192]{1,0:T(8,128)} %wgt_ref.1, s32[6,8192]{1,0:T(8,128)} %add_select_fusion.con_ref, s32[1,8192]{1,0:T(1,128)} %bitcast.84, s32[1,8192]{1,0:T(1,128)} %bitcast.85), custom_call_target="tpu_custom_call" | custom-call | flops 3221225472 | bytes 40000000 | tf_op jit(solution)/shard_map/pallas_call | solution.py:197
  34.1 2.0 copy.103
  36.1 3.1 all-to-all-start
  41.6 3.7 %collective-permute-start.2 = (f32[26,5,512]{2,0,1:T(8,128)S(1)}, f32[26,5,512]{2,0,1:T(8,128)S(1)}, u32[]{:S(2)}, u32[]{:S(2)}) collective-permute-start(f32[26,5,512]{2,0,1:T(8,128)S(1)} %copy.122), channel_id=1, source_target_pairs={{0,4},{4,8},{8,12},{1,5},{5,9},{9,13},{2,6},{6,10},{10,14},{3,7},{... | collective-permute-start | bytes 798728 | tf_op jit(solution)/shard_map/ppermute | solution.py:27
  46.2 1.3 collective-permute-start.3
  47.5 2.7 all-to-all-done
  52.7 46.5 %shard_map.105 = f32[512,512]{1,0:T(8,128)} custom-call(f32[512,512]{1,0:T(8,128)} %bitcast.82, f32[32,1,1024]{2,1,0:T(1,128)} %copy.104.val_ref, s32[32,1,1024]{2,1,0:T(1,128)} %copy.105.row_ref, s32[32,1,1024]{2,1,0:T(1,128)} %broadcast_in_dim.18.col_ref), custom_call_target="tpu_custom_call" | custom-call | flops 34359738368 | bytes 4000000 | tf_op jit(solution)/shard_map/pallas_call | solution.py:251
  100.3 2.0 collective-permute-start.8
  102.3 1.3 collective-permute-start.9
  103.7 7.6 %copy.98 = f32[26,32,512]{1,0,2:T(8,128)} copy(f32[26,32,512]{2,1,0:T(8,128)S(1)} %constant_dynamic-update-slice_fusion) | data formatting | bytes 3407872 | tf_op jit(solution)/shard_map/concatenate | solution.py:25
  111.3 7.5 %copy.97 = f32[26,5,512]{1,0,2:T(8,128)} copy(f32[26,5,512]{2,0,1:T(8,128)S(1)} %collective-permute-done.2) | data formatting | bytes 532480 | tf_op jit(solution)/shard_map/ppermute | solution.py:27
  118.8 7.6 %copy.99 = f32[26,5,512]{1,0,2:T(8,128)} copy(f32[26,5,512]{2,0,1:T(8,128)S(1)} %collective-permute-done.3) | data formatting | bytes 532480 | tf_op jit(solution)/shard_map/ppermute | solution.py:29
  126.5 1.3 pad_maximum_fusion.5
  128.0 3.0 collective-permute-start.10
  131.1 1.3 collective-permute-start.11
  132.4 10.5 %pad_maximum_fusion = f32[26,42,512]{1,0,2:T(8,128)S(1)} fusion(f32[26,5,512]{1,0,2:T(8,128)} %copy.99, f32[26,32,512]{1,0,2:T(8,128)} %copy.98, f32[26,5,512]{1,0,2:T(8,128)} %copy.97), kind=kLoop, calls=%fused_computation | loop fusion | flops 1118208 | bytes 4472832 | tf_op jit(solution)/shard_map/concatenate | solution.py:25
  142.9 3.3 %copy-done.4 = f32[26,42,512]{1,0,2:T(8,128)} copy-done((f32[26,42,512]{1,0,2:T(8,128)}, f32[26,42,512]{1,0,2:T(8,128)S(1)}, u32[]{:S(2)}) %copy-start.4) | copy-done | bytes 2236440
  146.2 3.1 collective-permute-start.4
  149.4 13.9 %collective-permute-start.5 = (f32[26,42,5]{1,0,2:T(8,128)S(1)}, f32[26,42,5]{1,0,2:T(8,128)S(1)}, u32[]{:S(2)}, u32[]{:S(2)}) collective-permute-start(f32[26,42,5]{1,0,2:T(8,128)S(1)} %get-tuple-element.28), channel_id=1, source_target_pairs={{1,0},{2,1},{3,2},{5,4},{6,5},{7,6},{9,8},{10,9},{11,10},{13,12},{... | collective-permute-start | bytes 65528 | tf_op jit(solution)/shard_map/ppermute | solution.py:29
  163.3 7.6 %copy.109 = f32[26,32,512]{1,0,2:T(8,128)} copy(f32[26,32,512]{2,1,0:T(8,128)S(1)} %pad_maximum_fusion.5) | data formatting | bytes 3407872 | tf_op jit(solution)/shard_map/concatenate | solution.py:25
  170.9 7.5 %copy.108 = f32[26,5,512]{1,0,2:T(8,128)} copy(f32[26,5,512]{2,0,1:T(8,128)S(1)} %collective-permute-done.10) | data formatting | bytes 532480 | tf_op jit(solution)/shard_map/ppermute | solution.py:27
  178.4 7.5 %copy.110 = f32[26,5,512]{1,0,2:T(8,128)} copy(f32[26,5,512]{2,0,1:T(8,128)S(1)} %collective-permute-done.11) | data formatting | bytes 532480 | tf_op jit(solution)/shard_map/ppermute | solution.py:29
  185.9 10.5 %pad_maximum_fusion.1 = f32[26,42,512]{1,0,2:T(8,128)S(1)} fusion(f32[26,5,512]{1,0,2:T(8,128)} %copy.110, f32[26,32,512]{1,0,2:T(8,128)} %copy.109, f32[26,5,512]{1,0,2:T(8,128)} %copy.108), kind=kLoop, calls=%fused_computation.1 | loop fusion | flops 1118208 | bytes 4472832 | tf_op jit(solution)/shard_map/concatenate | solution.py:25
  196.4 3.3 %copy-done.5 = f32[26,42,512]{1,0,2:T(8,128)} copy-done((f32[26,42,512]{1,0,2:T(8,128)}, f32[26,42,512]{1,0,2:T(8,128)S(1)}, u32[]{:S(2)}) %copy-start.5) | copy-done | bytes 2236440
  199.8 4.6 %collective-permute-start.12 = (f32[26,42,5]{1,0,2:T(8,128)S(1)}, f32[26,42,5]{1,0,2:T(8,128)S(1)}, u32[]{:S(2)}, u32[]{:S(2)}) collective-permute-start(f32[26,42,5]{1,0,2:T(8,128)S(1)} %get-tuple-element.25), channel_id=1, source_target_pairs={{0,1},{1,2},{2,3},{4,5},{5,6},{6,7},{8,9},{9,10},{10,11},{12,13},{... | collective-permute-start | bytes 65528 | tf_op jit(solution)/shard_map/ppermute | solution.py:27
  204.3 1.3 collective-permute-start.13
  206.1 7.1 %copy.101 = f32[26,42,512]{2,1,0:T(8,128)} copy(f32[26,42,512]{1,0,2:T(8,128)} %copy-done.4) | data formatting | bytes 4472832 | tf_op jit(solution)/shard_map/concatenate | solution.py:25
  213.3 2.1 copy.100
  216.5 7.1 %copy.112 = f32[26,42,512]{2,1,0:T(8,128)} copy(f32[26,42,512]{1,0,2:T(8,128)} %copy-done.5) | data formatting | bytes 4472832 | tf_op jit(solution)/shard_map/concatenate | solution.py:25
  223.7 1.2 copy.111
  224.9 1.2 copy.113
  226.0 4.8 %multiply_multiply_fusion.2 = (f32[26,42,522]{2,1,0:T(8,128)S(1)}, f32[26,42,522]{2,1,0:T(8,128)S(1)}, f32[26,42,522]{2,1,0:T(8,128)S(1)}) fusion(f32[26,42,5]{2,1,0:T(8,128)} %copy.102, f32[26,42,512]{2,1,0:T(8,128)} %copy.101, f32[26,42,5]{2,1,0:T(8,128)} %copy.100, f32[26,42,5]{2,1,0:T(8,128)} %copy.113, f32[26,42,512]{2,1,0:T(8,128)} %copy.112, ...), kind=kLoop, calls=%fused_computation.25 | loop fusion | flops 4560192 | bytes 11400480 | tf_op jit(solution)/shard_map/div | solution.py:52
  230.9 5.6 %multiply_add_fusion = (f32[26,42,522]{2,1,0:T(8,128)}, f32[26,42,522]{2,1,0:T(8,128)}) fusion(f32[26,42,522]{2,1,0:T(8,128)S(1)} %get-tuple-element.24, f32[26,42,522]{2,1,0:T(8,128)S(1)} %get-tuple-element.23, f32[522]{0:T(1024)S(1)} %fusion.96, f32[26,42]{1,0:T(8,128)S(1)} %broadcast_multiply_fusion.2, f32[26,42,522]{2,1,0:T(8,128)S(1)} %get-tuple-element.22), kind=kLoop, calls=%fused_computation.24 | loop fusion | flops 10830456 | bytes 11406936 | tf_op jit(solution)/shard_map/add | solution.py:64
  236.5 12.9 %fusion.4 = f32[26,42,522]{2,1,0:T(8,128)S(1)} fusion(f32[26,42,522]{2,1,0:T(8,128)} %get-tuple-element.20, f32[26,42,522]{2,1,0:T(8,128)S(1)} %get-tuple-element.24, f32[26,42,522]{2,1,0:T(8,128)} %get-tuple-element.21, f32[26,42,522]{2,1,0:T(8,128)S(1)} %get-tuple-element.23, f32[522]{0:T(1024)S(1)} %fusion.96, f32[26,42]{1,0:T(8,128)S(1)} %broadcast_multiply_fusion.2), kind=kLoop, calls=%fused_computation.8 | loop fusion | flops 9690408 | bytes 11406936 | tf_op jit(solution)/shard_map/add | solution.py:64
  249.4 2.0 bitcast_reduce_fusion.1
  253.6 2.6 collective-permute-start.14
  256.2 1.3 collective-permute-start.15
  257.6 1.9 collective-permute-done.15
  259.6 4.9 %collective-permute-start.16 = (f32[2,18,5,256]{3,2,1,0:T(8,128)S(1)}, f32[2,18,5,256]{3,2,1,0:T(8,128)S(1)}, u32[]{:S(2)}, u32[]{:S(2)}) collective-permute-start(f32[2,18,5,256]{3,2,1,0:T(8,128)S(1)} %get-tuple-element.43), channel_id=1, source_target_pairs={{0,4},{4,8},{8,12},{1,5},{5,9},{9,13},{2,6},{6,10},{10,14},{3,7},{... | collective-permute-start | bytes 552968 | tf_op jit(solution)/shard_map/ppermute | solution.py:27
  264.5 1.3 collective-permute-start.17
  265.9 5.2 %collective-permute-done.16 = f32[2,18,5,256]{3,2,1,0:T(8,128)S(1)} collective-permute-done((f32[2,18,5,256]{3,2,1,0:T(8,128)S(1)}, f32[2,18,5,256]{3,2,1,0:T(8,128)S(1)}, u32[]{:S(2)}, u32[]{:S(2)}) %collective-permute-start.16) | collective-permute-done | bytes 184352 | tf_op jit(solution)/shard_map/ppermute | solution.py:27
  271.0 9.4 %collective-permute-done.17 = f32[2,18,5,256]{3,2,1,0:T(8,128)S(1)} collective-permute-done((f32[2,18,5,256]{3,2,1,0:T(8,128)S(1)}, f32[2,18,5,256]{3,2,1,0:T(8,128)S(1)}, u32[]{:S(2)}, u32[]{:S(2)}) %collective-permute-start.17) | collective-permute-done | bytes 184352 | tf_op jit(solution)/shard_map/ppermute | solution.py:29
  280.6 1.2 fusion.119
  281.8 2.0 copy.116
  283.8 4.9 %collective-permute-start.18 = (f32[2,18,26,5]{2,0,3,1:T(2,128)}, f32[2,18,26,5]{2,0,3,1:T(2,128)}, u32[]{:S(2)}, u32[]{:S(2)}) collective-permute-start(f32[2,18,26,5]{2,0,3,1:T(2,128)} %copy.116), channel_id=1, source_target_pairs={{0,1},{1,2},{2,3},{4,5},{5,6},{6,7},{8,9},{9,10},{10,11},{12,13},{... | collective-permute-start | bytes 56168 | tf_op jit(solution)/shard_map/ppermute | solution.py:27
  288.7 2.0 copy.117
  290.7 1.5 collective-permute-start.19
  292.2 2.0 copy.118
  294.3 3.2 collective-permute-done.19
  297.5 2.0 copy.119
  299.5 2.5 pad_maximum_fusion.4
  305.1 1.4 fusion.54
  306.6 1.4 fusion.79
  308.1 1.7 copy-done.3
  310.6 1.2 copy-done.1
  311.8 4.8 %fusion.110 = (f32[22,38,518]{2,1,0:T(8,128)S(1)}, f32[22,38,518]{2,1,0:T(8,128)S(1)}, f32[22,38,518]{2,1,0:T(8,128)S(1)}, f32[22,38,518]{2,1,0:T(8,128)}, f32[22,38,518]{2,1,0:T(8,128)}) fusion(f32[22,38,518]{2,1,0:T(8,128)S(1)} %slice_add_fusion.1, f32[518]{0:T(1024)S(1)} %fusion.98, f32[22,38]{1,0:T(8,128)S(1)} %broadcast_multiply_fusion.3, ...), kind=kLoop, calls=%fused_computation.243 | loop fusion | flops 6495720 | bytes 13862952 | tf_op jit(solution)/shard_map/add | solution.py:57
  316.5 3.3 %fusion.109 = (f32[22,38,518]{2,1,0:T(8,128)S(1)}, f32[22,38,518]{2,1,0:T(8,128)S(1)}) fusion(f32[22,38,518]{2,1,0:T(8,128)S(1)} %get-tuple-element.14, f32[518]{0:T(1024)S(1)} %fusion.98, f32[22,38]{1,0:T(8,128)S(1)} %broadcast_multiply_fusion.3, f32[26,42,522]{2,1,0:T(8,128)S(1)} %copy-done.1, f32[26,42,522]{2,1,0:T(8,128)S(1)} %get-tuple-element.23, ...), kind=kLoop, calls=%fused_computation.242 | loop fusion | flops 7361816 | bytes 10398568 | tf_op jit(solution)/shard_map/add | solution.py:64
  319.9 2.3 add_subtract_fusion
  322.2 5.3 %slice_add_fusion.2 = f32[16,32,512]{2,1,0:T(8,128)} fusion(f32[22,38,518]{2,1,0:T(8,128)S(1)} %get-tuple-element.12, f32[22,38,518]{2,1,0:T(8,128)S(1)} %get-tuple-element.13, f32[22,38,518]{2,1,0:T(8,128)} %get-tuple-element.51, f32[22,38,518]{2,1,0:T(8,128)} %get-tuple-element.30, f32[22,38,518]{2,1,0:T(8,128)S(1)} %add_subtract_fusion, ...), kind=kLoop, calls=%fused_computation.59 | loop fusion | flops 1835008 | bytes 7340032 | tf_op jit(solution)/shard_map/add | solution.py:64
  (113 shorter events, 21.0 us)
Async XLA Ops:
  1.4 15.8 %collective-permute-start.6 = (f32[3,64]{1,0:T(4,128)S(1)}, f32[3,64]{1,0:T(4,128)S(1)}, u32[]{:S(2)}, u32[]{:S(2)}) collective-permute-start(f32[3,64]{1,0:T(4,128)S(1)} %get-tuple-element.50), channel_id=1, source_target_pairs={{0,1},{1,2},{2,3},{3,4},{4,5},{5,6},{6,7},{7,8},{8,9},{9,10},{10,1... | collective-permute-start | bytes 2312 | tf_op jit(solution)/shard_map/ppermute | solution.py:27
  4.5 12.8 %collective-permute-start.7 = (f32[3,64]{1,0:T(4,128)S(1)}, f32[3,64]{1,0:T(4,128)S(1)}, u32[]{:S(2)}, u32[]{:S(2)}) collective-permute-start(f32[3,64]{1,0:T(4,128)S(1)} %get-tuple-element.49), channel_id=1, source_target_pairs={{1,0},{2,1},{3,2},{4,3},{5,4},{6,5},{7,6},{8,7},{9,8},{10,9},{11,1... | collective-permute-start | bytes 2312 | tf_op jit(solution)/shard_map/ppermute | solution.py:29
  9.0 30.3 %collective-permute-start = (f32[5,32,512]{2,1,0:T(8,128)S(1)}, f32[5,32,512]{2,1,0:T(8,128)}, u32[]{:S(2)}, u32[]{:S(2)}) collective-permute-start(f32[5,32,512]{2,1,0:T(8,128)S(1)} %get-tuple-element.42), channel_id=1, source_target_pairs={{0,16},{1,17},{2,18},{3,19},{4,20},{5,21},{6,22},{7,23},{8,24},{9,... | collective-permute-start | bytes 983048 | tf_op jit(solution)/shard_map/ppermute | solution.py:27
  12.3 28.1 %collective-permute-start.1 = (f32[5,32,512]{2,1,0:T(8,128)S(1)}, f32[5,32,512]{2,1,0:T(8,128)}, u32[]{:S(2)}, u32[]{:S(2)}) collective-permute-start(f32[5,32,512]{2,1,0:T(8,128)S(1)} %get-tuple-element.41), channel_id=1, source_target_pairs={{16,0},{17,1},{18,2},{19,3},{20,4},{21,5},{22,6},{23,7},{24,8},{25... | collective-permute-start | bytes 983048 | tf_op jit(solution)/shard_map/ppermute | solution.py:29
  14.2 238.2 %copy-start.16 = (s32[256]{0:T(256)}, s32[256]{0:T(256)S(1)}, u32[]{:S(2)}) copy-start(s32[256]{0:T(256)S(1)} %get-tuple-element.55) | copy-start | bytes 3076
  14.2 238.2 %copy-start.17 = (s32[256]{0:T(256)}, s32[256]{0:T(256)S(1)}, u32[]{:S(2)}) copy-start(s32[256]{0:T(256)S(1)} %get-tuple-element.56) | copy-start | bytes 3076
  14.2 238.2 %copy-start.18 = (pred[256]{0:T(512)(128)(4,1)}, pred[256]{0:T(512)(128)(4,1)S(1)}, u32[]{:S(2)}) copy-start(pred[256]{0:T(512)(128)(4,1)S(1)} %compare_and_fusion) | copy-start | bytes 772
  34.1 6.1 %copy-start.6 = (f32[16,32,512]{2,1,0:T(8,128)S(1)}, f32[16,32,512]{2,1,0:T(8,128)}, u32[]{:S(2)}) copy-start(f32[16,32,512]{2,1,0:T(8,128)} %param.10) | copy-start | bytes 3145732
  36.1 14.0 %all-to-all-start = ((f32[32,1,2048]{2,1,0:T(1,128)}), f32[32,1,2048]{2,1,0:T(1,128)S(1)}, u32[]{:S(2)}, u32[]{:S(2)}) async-start(f32[32,1,2048]{2,1,0:T(1,128)} %copy.103), calls=%async_computation | async-start | bytes 524288 | tf_op jit(solution)/shard_map/all_to_all | solution.py:286
  41.6 69.7 %collective-permute-start.2 = (f32[26,5,512]{2,0,1:T(8,128)S(1)}, f32[26,5,512]{2,0,1:T(8,128)S(1)}, u32[]{:S(2)}, u32[]{:S(2)}) collective-permute-start(f32[26,5,512]{2,0,1:T(8,128)S(1)} %copy.122), channel_id=1, source_target_pairs={{0,4},{4,8},{8,12},{1,5},{5,9},{9,13},{2,6},{6,10},{10,14},{3,7},{... | collective-permute-start | bytes 798728 | tf_op jit(solution)/shard_map/ppermute | solution.py:27
  46.2 72.6 %collective-permute-start.3 = (f32[26,5,512]{2,0,1:T(8,128)}, f32[26,5,512]{2,0,1:T(8,128)S(1)}, u32[]{:S(2)}, u32[]{:S(2)}) collective-permute-start(f32[26,5,512]{2,0,1:T(8,128)} %copy.123), channel_id=1, source_target_pairs={{4,0},{8,4},{12,8},{5,1},{9,5},{13,9},{6,2},{10,6},{14,10},{7,3},{... | collective-permute-start | bytes 798728 | tf_op jit(solution)/shard_map/ppermute | solution.py:29
  100.3 26.2 %collective-permute-start.8 = (f32[5,32,512]{2,1,0:T(8,128)S(1)}, f32[5,32,512]{2,1,0:T(8,128)}, u32[]{:S(2)}, u32[]{:S(2)}) collective-permute-start(f32[5,32,512]{2,1,0:T(8,128)S(1)} %bitcast.80), channel_id=1, source_target_pairs={{0,16},{1,17},{2,18},{3,19},{4,20},{5,21},{6,22},{7,23},{8,24},{9,... | collective-permute-start | bytes 983048 | tf_op jit(solution)/shard_map/ppermute | solution.py:27
  102.3 24.2 %collective-permute-start.9 = (f32[5,32,512]{2,1,0:T(8,128)S(1)}, f32[5,32,512]{2,1,0:T(8,128)}, u32[]{:S(2)}, u32[]{:S(2)}) collective-permute-start(f32[5,32,512]{2,1,0:T(8,128)S(1)} %bitcast.79), channel_id=1, source_target_pairs={{16,0},{17,1},{18,2},{19,3},{20,4},{21,5},{22,6},{23,7},{24,8},{25... | collective-permute-start | bytes 983048 | tf_op jit(solution)/shard_map/ppermute | solution.py:29
  118.8 7.6 %copy-start.8 = (f32[512,512]{1,0:T(8,128)S(1)}, f32[512,512]{1,0:T(8,128)}, u32[]{:S(2)}) copy-start(f32[512,512]{1,0:T(8,128)} %shard_map.105) | copy-start | bytes 3145732
  128.0 42.9 %collective-permute-start.10 = (f32[26,5,512]{2,0,1:T(8,128)S(1)}, f32[26,5,512]{2,0,1:T(8,128)S(1)}, u32[]{:S(2)}, u32[]{:S(2)}) collective-permute-start(f32[26,5,512]{2,0,1:T(8,128)S(1)} %copy.124), channel_id=1, source_target_pairs={{0,4},{4,8},{8,12},{1,5},{5,9},{9,13},{2,6},{6,10},{10,14},{3,7},{... | collective-permute-start | bytes 798728 | tf_op jit(solution)/shard_map/ppermute | solution.py:27
  131.1 47.3 %collective-permute-start.11 = (f32[26,5,512]{2,0,1:T(8,128)S(1)}, f32[26,5,512]{2,0,1:T(8,128)S(1)}, u32[]{:S(2)}, u32[]{:S(2)}) collective-permute-start(f32[26,5,512]{2,0,1:T(8,128)S(1)} %copy.125), channel_id=1, source_target_pairs={{4,0},{8,4},{12,8},{5,1},{9,5},{13,9},{6,2},{10,6},{14,10},{7,3},{... | collective-permute-start | bytes 798728 | tf_op jit(solution)/shard_map/ppermute | solution.py:29
  142.9 3.3 %copy-start.4 = (f32[26,42,512]{1,0,2:T(8,128)}, f32[26,42,512]{1,0,2:T(8,128)S(1)}, u32[]{:S(2)}) copy-start(f32[26,42,512]{1,0,2:T(8,128)S(1)} %pad_maximum_fusion) | copy-start | bytes 6709252
  146.2 67.0 %collective-permute-start.4 = (f32[26,42,5]{1,0,2:T(8,128)S(1)}, f32[26,42,5]{1,0,2:T(8,128)}, u32[]{:S(2)}, u32[]{:S(2)}) collective-permute-start(f32[26,42,5]{1,0,2:T(8,128)S(1)} %get-tuple-element.27), channel_id=1, source_target_pairs={{0,1},{1,2},{2,3},{4,5},{5,6},{6,7},{8,9},{9,10},{10,11},{12,13},{... | collective-permute-start | bytes 65528 | tf_op jit(solution)/shard_map/ppermute | solution.py:27
  149.4 65.9 %collective-permute-start.5 = (f32[26,42,5]{1,0,2:T(8,128)S(1)}, f32[26,42,5]{1,0,2:T(8,128)S(1)}, u32[]{:S(2)}, u32[]{:S(2)}) collective-permute-start(f32[26,42,5]{1,0,2:T(8,128)S(1)} %get-tuple-element.28), channel_id=1, source_target_pairs={{1,0},{2,1},{3,2},{5,4},{6,5},{7,6},{9,8},{10,9},{11,10},{13,12},{... | collective-permute-start | bytes 65528 | tf_op jit(solution)/shard_map/ppermute | solution.py:29
  196.4 3.3 %copy-start.5 = (f32[26,42,512]{1,0,2:T(8,128)}, f32[26,42,512]{1,0,2:T(8,128)S(1)}, u32[]{:S(2)}) copy-start(f32[26,42,512]{1,0,2:T(8,128)S(1)} %pad_maximum_fusion.1) | copy-start | bytes 6709252
  199.8 23.9 %collective-permute-start.12 = (f32[26,42,5]{1,0,2:T(8,128)S(1)}, f32[26,42,5]{1,0,2:T(8,128)S(1)}, u32[]{:S(2)}, u32[]{:S(2)}) collective-permute-start(f32[26,42,5]{1,0,2:T(8,128)S(1)} %get-tuple-element.25), channel_id=1, source_target_pairs={{0,1},{1,2},{2,3},{4,5},{5,6},{6,7},{8,9},{9,10},{10,11},{12,13},{... | collective-permute-start | bytes 65528 | tf_op jit(solution)/shard_map/ppermute | solution.py:27
  204.3 20.5 %collective-permute-start.13 = (f32[26,42,5]{1,0,2:T(8,128)S(1)}, f32[26,42,5]{1,0,2:T(8,128)S(1)}, u32[]{:S(2)}, u32[]{:S(2)}) collective-permute-start(f32[26,42,5]{1,0,2:T(8,128)S(1)} %get-tuple-element.26), channel_id=1, source_target_pairs={{1,0},{2,1},{3,2},{5,4},{6,5},{7,6},{9,8},{10,9},{11,10},{13,12},{... | collective-permute-start | bytes 65528 | tf_op jit(solution)/shard_map/ppermute | solution.py:29
  230.9 5.6 %copy-start = (f32[26,42,522]{2,1,0:T(8,128)}, f32[26,42,522]{2,1,0:T(8,128)S(1)}, u32[]{:S(2)}) copy-start(f32[26,42,522]{2,1,0:T(8,128)S(1)} %get-tuple-element.24) | copy-start | bytes 6840292
  236.5 12.9 %copy-start.7 = (f32[16,32,512]{2,1,0:T(8,128)S(1)}, f32[16,32,512]{2,1,0:T(8,128)}, u32[]{:S(2)}) copy-start(f32[16,32,512]{2,1,0:T(8,128)} %param.10) | copy-start | bytes 3145732
  236.5 12.9 %copy-start.9 = (f32[512,512]{1,0:T(8,128)S(1)}, f32[512,512]{1,0:T(8,128)}, u32[]{:S(2)}) copy-start(f32[512,512]{1,0:T(8,128)} %shard_map.105) | copy-start | bytes 3145732
  249.4 2.1 copy-start.2
  249.4 2.1 copy-start.19
  251.9 13.9 %copy-start.20 = (f32[38]{0:T(128)S(1)}, f32[38]{0:T(128)}, u32[]{:S(2)}) copy-start(f32[38]{0:T(128)} %and_convert_fusion) | copy-start | bytes 460
  253.6 4.0 %collective-permute-start.14 = (f32[2,5,16,256]{3,2,1,0:T(8,128)S(1)}, f32[2,5,16,256]{3,2,1,0:T(8,128)S(1)}, u32[]{:S(2)}, u32[]{:S(2)}) collective-permute-start(f32[2,5,16,256]{3,2,1,0:T(8,128)S(1)} %get-tuple-element.45), channel_id=1, source_target_pairs={{0,16},{1,17},{2,18},{3,19},{4,20},{5,21},{6,22},{7,23},{8,24},{9,... | collective-permute-start | bytes 491528 | tf_op jit(solution)/shard_map/ppermute | solution.py:27
  256.2 3.3 %collective-permute-start.15 = (f32[2,5,16,256]{3,2,1,0:T(8,128)S(1)}, f32[2,5,16,256]{3,2,1,0:T(8,128)S(1)}, u32[]{:S(2)}, u32[]{:S(2)}) collective-permute-start(f32[2,5,16,256]{3,2,1,0:T(8,128)S(1)} %get-tuple-element.46), channel_id=1, source_target_pairs={{16,0},{17,1},{18,2},{19,3},{20,4},{21,5},{22,6},{23,7},{24,8},{25... | collective-permute-start | bytes 491528 | tf_op jit(solution)/shard_map/ppermute | solution.py:29
  257.6 23.1 %copy-start.10 = (f32[2,5,16,256]{3,2,1,0:T(8,128)}, f32[2,5,16,256]{3,2,1,0:T(8,128)S(1)}, u32[]{:S(2)}) copy-start(f32[2,5,16,256]{3,2,1,0:T(8,128)S(1)} %collective-permute-done.14) | copy-start | bytes 491524
  259.5 21.1 %copy-start.11 = (f32[2,5,16,256]{3,2,1,0:T(8,128)}, f32[2,5,16,256]{3,2,1,0:T(8,128)S(1)}, u32[]{:S(2)}) copy-start(f32[2,5,16,256]{3,2,1,0:T(8,128)S(1)} %collective-permute-done.15) | copy-start | bytes 491524
  259.6 11.4 %collective-permute-start.16 = (f32[2,18,5,256]{3,2,1,0:T(8,128)S(1)}, f32[2,18,5,256]{3,2,1,0:T(8,128)S(1)}, u32[]{:S(2)}, u32[]{:S(2)}) collective-permute-start(f32[2,18,5,256]{3,2,1,0:T(8,128)S(1)} %get-tuple-element.43), channel_id=1, source_target_pairs={{0,4},{4,8},{8,12},{1,5},{5,9},{9,13},{2,6},{6,10},{10,14},{3,7},{... | collective-permute-start | bytes 552968 | tf_op jit(solution)/shard_map/ppermute | solution.py:27
  264.5 15.9 %collective-permute-start.17 = (f32[2,18,5,256]{3,2,1,0:T(8,128)S(1)}, f32[2,18,5,256]{3,2,1,0:T(8,128)S(1)}, u32[]{:S(2)}, u32[]{:S(2)}) collective-permute-start(f32[2,18,5,256]{3,2,1,0:T(8,128)S(1)} %get-tuple-element.44), channel_id=1, source_target_pairs={{4,0},{8,4},{12,8},{5,1},{9,5},{13,9},{6,2},{10,6},{14,10},{7,3},{... | collective-permute-start | bytes 552968 | tf_op jit(solution)/shard_map/ppermute | solution.py:29
  271.0 10.8 %copy-start.12 = (f32[2,18,5,256]{3,2,1,0:T(8,128)}, f32[2,18,5,256]{3,2,1,0:T(8,128)S(1)}, u32[]{:S(2)}) copy-start(f32[2,18,5,256]{3,2,1,0:T(8,128)S(1)} %collective-permute-done.16) | copy-start | bytes 552964
  280.4 1.4 copy-start.13
  283.8 8.4 %collective-permute-start.18 = (f32[2,18,26,5]{2,0,3,1:T(2,128)}, f32[2,18,26,5]{2,0,3,1:T(2,128)}, u32[]{:S(2)}, u32[]{:S(2)}) collective-permute-start(f32[2,18,26,5]{2,0,3,1:T(2,128)} %copy.116), channel_id=1, source_target_pairs={{0,1},{1,2},{2,3},{4,5},{5,6},{6,7},{8,9},{9,10},{10,11},{12,13},{... | collective-permute-start | bytes 56168 | tf_op jit(solution)/shard_map/ppermute | solution.py:27
  290.7 6.8 %collective-permute-start.19 = (f32[2,18,26,5]{2,0,3,1:T(2,128)}, f32[2,18,26,5]{2,0,3,1:T(2,128)}, u32[]{:S(2)}, u32[]{:S(2)}) collective-permute-start(f32[2,18,26,5]{2,0,3,1:T(2,128)} %copy.117), channel_id=1, source_target_pairs={{1,0},{2,1},{3,2},{5,4},{6,5},{7,6},{9,8},{10,9},{11,10},{13,12},{... | collective-permute-start | bytes 56168 | tf_op jit(solution)/shard_map/ppermute | solution.py:29
  302.1 0.6 copy-start.15
  305.1 1.5 copy-start.14
  308.0 1.9 copy-start.3
  309.9 1.9 copy-start.1

commit v2 on v1

--- a/solution.py
+++ b/solution.py
@@ -16,8 +16,8 @@
 spread = 0.875
 
 
-def padded_2(cells, sides, width, closed):
-    for axis, dim in sides:
+def padded_2(cells, sides, closed):
+    for axis, dim, width in sides:
         count = lax.axis_size(axis)
         ends = count if closed else count - 1
         head = lax.slice_in_dim(cells, 0, width, axis=dim)
@@ -33,52 +33,131 @@
     return cells
 
 
-def stencil(padded, field, shift):
-    beside = padded[2:, 1:-1, 1:-1] + padded[:-2, 1:-1, 1:-1]
-    beside = beside + padded[1:-1, 2:, 1:-1] + padded[1:-1, :-2, 1:-1]
-    beside = beside + padded[1:-1, 1:-1, 2:] + padded[1:-1, 1:-1, :-2]
-    return (6.0 + shift) * field - beside
-
-
-def local_apply(field, shift):
-    return stencil(jnp.pad(field, 1), field, shift)
-
-
-def chebyshev(target, shift, start, sweeps, apply_fn, inside):
-    inverse = 1.0 / (6.0 + shift)
+def factors(sweeps):
     ratio = centre / spread
-    factor = 1.0 / ratio
-    if start is None:
-        update = inverse * target / centre
-        answer = update
-    else:
-        update = inverse * (target - apply_fn(start, shift)) / centre
-        update = update * inside
-        answer = start + update
-    for sweep in range(1, sweeps):
-        remain = inverse * (target - apply_fn(answer, shift))
-        if inside is not None:
-            remain = remain * inside
-        factor_new = 1.0 / (2.0 * ratio - factor)
-        update = factor_new * factor * update + 2.0 * factor_new / spread * remain
-        answer = answer + update
-        factor = factor_new
-    return answer
-
-
-def domain_mask(shape, width):
-    places = (lax.axis_index("gx"), lax.axis_index("gy"), lax.axis_index("gz"))
-    counts = (lax.axis_size("gx"), lax.axis_size("gy"), lax.axis_size("gz"))
-    factors = []
-    for which in range(3):
-        length = shape[which]
-        where = places[which] * length - width + jnp.arange(length + 2 * width, dtype=jnp.int32)
-        factors.append(((where >= 0) & (where < length * counts[which])).astype(jnp.float32))
-    return factors[0][:, None, None] * factors[1][None, :, None] * factors[2][None, None, :]
-
-
-def interior(field, width):
-    return field[width:-width, width:-width, width:-width]
+    fac = 1.0 / ratio
+    pairs = [(0.0, 1.0 / centre)]
+    for _ in range(1, sweeps):
+        fac_new = 1.0 / (2.0 * ratio - fac)
+        pairs.append((fac_new * fac, 2.0 * fac_new / spread))
+        fac = fac_new
+    return pairs
+
+
+def beside(ref, x, cells):
+    ny, nz = cells.shape
+    total = ref[x - 1] + ref[x + 1]
+    total = total + pltpu.roll(cells, 1, 0) + pltpu.roll(cells, ny - 1, 0)
+    return total + pltpu.roll(cells, 1, 1) + pltpu.roll(cells, nz - 1, 1)
+
+
+def sweep(rhs, inverse, src, dst, update, first, last, pair, keep=None):
+    old, new = pair
+
+    def slab(x, carry):
+        cells = src[x]
+        change = new * (inverse[x] * (rhs[x] + beside(src, x, cells)) - cells)
+        if old:
+            change = change + old * update[x]
+        if keep is None:
+            update[x] = change
+            dst[x] = cells + change
+        else:
+            keep(x, cells + change)
+        return carry
+
+    lax.fori_loop(first, last, slab, 0)
+
+
+def begin(rhs, inverse, dst, update, slabs):
+    def slab(x, carry):
+        change = inverse[x] * rhs[x] * (1.0 / centre)
+        update[x] = change
+        dst[x] = change
+        return carry
+
+    lax.fori_loop(0, slabs, slab, 0)
+
+
+def down_kernel(wx, wy, wz, rhs, inverse, shift, smooth, remain, one, update):
+    slabs = rhs.shape[0]
+    ny, nz = remain.shape[1:]
+    pairs = factors(SMOOTH)
+    bufs = (one, smooth) if SMOOTH % 2 == 0 else (smooth, one)
+    begin(rhs, inverse, bufs[0], update, slabs)
+    for k in range(1, SMOOTH):
+        sweep(
+            rhs, inverse, bufs[(k - 1) % 2], bufs[k % 2], update, k, slabs - k, pairs[k]
+        )
+
+    def slab(x, carry):
+        cells = smooth[x]
+        near = rhs[x] + beside(smooth, x, cells)
+        core = (slice(wy, wy + ny), slice(wz, wz + nz))
+        remain[x - wx] = near[core] - (6.0 + shift[x - wx]) * cells[core]
+        return carry
+
+    lax.fori_loop(wx, slabs - wx, slab, 0)
+
+
+def up_kernel(
+    wx, wy, wz, cx, coarse, rhs, inverse, smooth, pressure,
+    fix_a, fix_b, fix_update, one, two, update,
+):
+    crhs, cinverse = coarse.at[0], coarse.at[1]
+    cslabs, cny, cnz = fix_a.shape
+    slabs, fny, fnz = one.shape
+    ny, nz = pressure.shape[1:]
+    pairs = factors(COARSE_SMOOTH)
+    bufs = (fix_a, fix_b)
+    begin(crhs, cinverse, fix_a, fix_update, cslabs)
+    for k in range(1, COARSE_SMOOTH):
+        sweep(
+            crhs, cinverse, bufs[(k - 1) % 2], bufs[k % 2], fix_update, k, cslabs - k, pairs[k]
+        )
+    fix = bufs[(COARSE_SMOOTH - 1) % 2]
+
+    low = cx - (SMOOTH + 1) // 2
+    count = cslabs - 2 * low
+    flat = fix[low : low + count].reshape(count * cny, cnz)
+
+    def onehot(shape, offset_f, offset_c, fine_dim, fine_per, coarse_per):
+        f = lax.broadcasted_iota(jnp.int32, shape, fine_dim)
+        c = lax.broadcasted_iota(jnp.int32, shape, 1 - fine_dim)
+        block, inner = 0, f
+        for g in range(1, shape[fine_dim] // fine_per):
+            block = block + (f >= g * fine_per).astype(jnp.int32)
+        inner = f - block * fine_per
+        half = jnp.right_shift(inner - offset_f + 2 * offset_c, 1)
+        return (c == half + block * coarse_per).astype(jnp.float32).astype(jnp.bfloat16)
+
+    fan_y = onehot((count * fny, count * cny), wy, wy, 0, fny, cny)
+    fan_z = onehot((cnz, fnz), wz, wz, 1, fnz, cnz)
+    tall = sum(
+        jnp.dot(fan_y, piece, preferred_element_type=jnp.float32) for piece in split3(flat)
+    )
+    full = sum(
+        jnp.dot(piece, fan_z, preferred_element_type=jnp.float32) for piece in split3(tall)
+    )
+    for j in range(count):
+        part = full[j * fny : (j + 1) * fny]
+        for half in range(2):
+            x = wx + 2 * (low + j - cx) + half
+            if wx - SMOOTH <= x < slabs - wx + SMOOTH:
+                one[x] = smooth[x] + part
+
+    pairs = factors(SMOOTH)
+    bufs = (one, two)
+
+    def keep(x, cells):
+        pressure[x - wx] = cells[wy : wy + ny, wz : wz + nz]
+
+    edge = wx - SMOOTH
+    for k in range(SMOOTH):
+        sweep(
+            rhs, inverse, bufs[k % 2], bufs[(k + 1) % 2], update,
+            edge + k + 1, slabs - edge - k - 1, pairs[k], keep if k == SMOOTH - 1 else None,
+        )
 
 
 LANES = 2 * HALO
@@ -100,20 +179,6 @@
         pair_matrix(nx // 2 * ny // 2, nx // 2 * ny), along_z, precision=HIGH
     )
     return along_y.reshape(nx // 2, ny // 2, nz // 2)
-
-
-def spread_out(coarse, crop):
-    nx, ny, nz = coarse.shape
-    along_z = jnp.dot(
-        coarse.reshape(nx * ny, nz), pair_matrix(nz, 2 * nz - 2 * crop, crop), precision=HIGH
-    ).reshape(nx, ny, 2 * nz - 2 * crop)
-    fan = jnp.broadcast_to(
-        pair_matrix(ny, 2 * ny - 2 * crop, crop).T[None], (nx, 2 * ny - 2 * crop, ny)
-    )
-    along_y = jnp.einsum("xyb,xbc->xyc", fan, along_z, precision=HIGH)
-    twice = jnp.broadcast_to(along_y[:, None], (nx, 2) + along_y.shape[1:])
-    twice = twice.reshape((2 * nx,) + along_y.shape[1:])
-    return twice[crop : 2 * nx - crop]
 
 
 def split3(x):
@@ -276,7 +341,7 @@
     ndevice = lax.axis_size(("gx", "gy", "gz"))
     total = npoint * ndevice
     begin = lax.axis_index(("gx", "gy", "gz")) * npoint
-    padded = padded_2(positions, ((("gx", "gy", "gz"), 1),), HALO, True)
+    padded = padded_2(positions, ((("gx", "gy", "gz"), 1, HALO),), True)
     relative = (connectivity - begin + HALO + total) % total
     capacity = 4 * npoint // ndevice
     surface_force, packed = points(
@@ -286,43 +351,36 @@
     got = lax.all_to_all(packed, ("gx", "gy", "gz"), split_axis=0, concat_axis=0, tiled=True)
     forcing = scatter(pressure_rhs, got[:, :capacity], got[:, capacity:].astype(jnp.int32))
 
-    sides = (("gx", 0), ("gy", 1), ("gz", 2))
-    shape = pressure_rhs.shape
+    nx, ny, nz = pressure_rhs.shape
+    wx, wy, wz = 2 * SMOOTH - 1, 8, 128
+    cx = COARSE_SMOOTH - 1 + (SMOOTH + 1) // 2
+    sides = (("gz", 2, wz), ("gy", 1, wy), ("gx", 0, wx))
+    coarse_sides = (("gz", 3, wz), ("gy", 2, wy), ("gx", 1, cx))
     coarse_shift = 0.5 * pool(shift_diag)
-    last = SMOOTH
-    width = SMOOTH + SMOOTH - 1
-    reach = (last + 1) // 2
-    coarse_width = COARSE_SMOOTH - 1 + reach
-    shift_wide = padded_2(shift_diag, sides, width, False)
-    forcing_wide = padded_2(forcing, sides, width, False)
-    smooth_wide = chebyshev(
-        forcing_wide, shift_wide, None, SMOOTH, local_apply, domain_mask(shape, width)
-    )
-    near = slice(width - 1, -(width - 1))
-    near = (near, near, near)
-    remain = interior(forcing_wide, width) - stencil(
-        smooth_wide[near], interior(smooth_wide, width), interior(shift_wide, width)
-    )
-    coarse_rhs = 0.5 * pool(remain)
-    coarse_sides = (("gx", 1), ("gy", 2), ("gz", 3))
-    coarse_wide = padded_2(
-        jnp.stack([coarse_rhs, coarse_shift]), coarse_sides, coarse_width, False
-    )
-    coarse_fix = chebyshev(
-        coarse_wide[0], coarse_wide[1], None, COARSE_SMOOTH, local_apply,
-        domain_mask(coarse_rhs.shape, coarse_width),
-    )
-    coarse_fix = interior(coarse_fix, coarse_width - reach)
-    spreadout = spread_out(coarse_fix, 2 * reach - last)
-    trim = width - last
-    start_wide = interior(smooth_wide, trim) + spreadout
-    pressure = interior(
-        chebyshev(
-            interior(forcing_wide, trim), interior(shift_wide, trim), start_wide, SMOOTH,
-            local_apply, domain_mask(shape, last),
-        ),
-        last,
-    )
+    inverse = padded_2(1.0 / (6.0 + shift_diag), sides, False)
+    rhs = padded_2(forcing, sides, False)
+    wide = jax.ShapeDtypeStruct(rhs.shape, jnp.float32)
+    core = jax.ShapeDtypeStruct(pressure_rhs.shape, jnp.float32)
+    vmem = pl.BlockSpec(memory_space=pltpu.VMEM)
+    wide_buf = pltpu.VMEM(rhs.shape, jnp.float32)
+    smooth, remain = pl.pallas_call(
+        functools.partial(down_kernel, wx, wy, wz),
+        in_specs=[vmem] * 3,
+        out_specs=[vmem] * 2,
+        out_shape=[wide, core],
+        scratch_shapes=[wide_buf] * 2,
+    )(rhs, inverse, shift_diag)
+    coarse = padded_2(
+        jnp.stack([0.5 * pool(remain), 1.0 / (6.0 + coarse_shift)]), coarse_sides, False
+    )
+    fix_buf = pltpu.VMEM(coarse.shape[1:], jnp.float32)
+    pressure = pl.pallas_call(
+        functools.partial(up_kernel, wx, wy, wz, cx),
+        in_specs=[vmem] * 4,
+        out_specs=vmem,
+        out_shape=core,
+        scratch_shapes=[fix_buf] * 3 + [wide_buf] * 3,
+    )(coarse, rhs, inverse, smooth)
     return (pressure, surface_force)
 
 

time: 332 us -> 221 us (0.67)
  local copies, waits for them, and re-layouts: 97.7 us -> 8.32 us
  other arithmetic: 73.7 us -> 9.97 us
  Pallas kernels: 61.5 us -> 98.8 us
  waiting for transfers between devices: 22.4 us -> 58.7 us
  starting transfers between devices: 65.9 us -> 41.9 us
  matrix products: 4.81 us -> 1.38 us
    ppermute x10 -> x0, local copies, waits for them, and re-layouts: 39.9 us -> none  [the longest x5 20.4 us: padded_2(): lax.ppermute(tail, axis, [(i, (i + 1) % count) for i in range(ends)])]
    pallas_call x0 -> x2, Pallas kernels: none -> 37.3 us  [the longest x1 21.9 us: body(): pl.pallas_call(functools.partial(up_kernel, wx, wy, wz, cx), in_specs=[vm...]
    add x8 -> x0, other arithmetic: 34.5 us -> none  [the longest x6 29 us: chebyshev(): answer = answer + update]
    concatenate x6 -> x1, local copies, waits for them, and re-layouts: 31.6 us -> 1.09 us  [padded_2(): jnp.concatenate([lax.ppermute(tail, axis, [(i, (i + 1) % count) for i in...]
    ppermute x10, waiting for transfers between devices: 14.6 us -> 40.4 us  [padded_2(): lax.ppermute(head, axis, [((i + 1) % count, i) for i in range(ends)])]
    concatenate x6 -> x5, other arithmetic: 25 us -> 6.16 us  [padded_2(): jnp.concatenate([lax.ppermute(tail, axis, [(i, (i + 1) % count) for i in...]
    ppermute x10, starting transfers between devices: 35.1 us -> 21.1 us  [padded_2(): lax.ppermute(tail, axis, [(i, (i + 1) % count) for i in range(ends)])]
    unnamed x49 -> x5, local copies, waits for them, and re-layouts: 12.5 us -> 0.09 us
  transfers between devices with their start and end apart: 21 -> 21, of which waited for: 5 -> 12; matrix products, arithmetic and copies ran while one was open for 32% -> 4% of each run, Pallas kernels for 19% -> 21%
where the time goes in v2:
time: 221 us; the launch traced here: 220 us
  Pallas kernels  98.8 us (45%)
  waiting for transfers between devices  58.7 us (27%)
  starting transfers between devices  41.9 us (19%)
  other arithmetic  9.97 us (5%)
  local copies, waits for them, and re-layouts  8.32 us (4%)
    pallas_call x1, Pallas kernels, scatter(): pl.pallas_call(scatter_kernel, grid=(sources,), in_specs=[whole, one, one...  46.5 us
    ppermute x10, waiting for transfers between devices, padded_2(): lax.ppermute(head, axis, [((i + 1) % count, i) for i in range(ends)])  40.4 us
    pallas_call x1, Pallas kernels, body(): pl.pallas_call(functools.partial(up_kernel, wx, wy, wz, cx), in_specs=[vm...  21.9 us
    ppermute x10, starting transfers between devices, padded_2(): lax.ppermute(tail, axis, [(i, (i + 1) % count) for i in range(ends)])  21.1 us
    ppermute x10, starting transfers between devices, padded_2(): lax.ppermute(head, axis, [((i + 1) % count, i) for i in range(ends)])  18.2 us
    pallas_call x1, Pallas kernels, body(): pl.pallas_call(functools.partial(down_kernel, wx, wy, wz), in_specs=[vmem...  15.4 us
    pallas_call x1, Pallas kernels, points(): pl.pallas_call(functools.partial(points_kernel, ndevice, capacity), grid=...  15.1 us
    ppermute x10, waiting for transfers between devices, padded_2(): lax.ppermute(tail, axis, [(i, (i + 1) % count) for i in range(ends)])  12.6 us
  transfers between devices with their start and end apart: 21, of which 12 were waited for; matrix products, arithmetic and copies ran while one was open for 4% of the time, Pallas kernels for 21%

profile of v2, /device:TPU:0, one launch (start us, length us, event | category | flops | bytes accessed | tf_op | source)
XLA Modules:
  0.0 220.2 jit_solution(13432621911680485201)
XLA Ops:
  0.6 0.8 fusion.28
  1.4 6.4 %collective-permute-start.1 = (f32[3,64]{1,0:T(4,128)S(1)}, f32[3,64]{1,0:T(4,128)S(1)}, u32[]{:S(2)}, u32[]{:S(2)}) collective-permute-start(f32[3,64]{1,0:T(4,128)S(1)} %get-tuple-element.30), channel_id=1, source_target_pairs={{1,0},{2,1},{3,2},{4,3},{5,4},{6,5},{7,6},{8,7},{9,8},{10,9},{11,1... | collective-permute-start | bytes 2312 | tf_op jit(solution)/shard_map/ppermute | solution.py:29
  7.8 1.8 add_select_fusion.con_ref
  9.6 4.8 %collective-permute-done = f32[3,64]{1,0:T(4,128)S(1)} collective-permute-done((f32[3,64]{1,0:T(4,128)S(1)}, f32[3,64]{1,0:T(4,128)S(1)}, u32[]{:S(2)}, u32[]{:S(2)}) %collective-permute-start) | collective-permute-done | bytes 800 | tf_op jit(solution)/shard_map/ppermute | solution.py:27
  14.4 1.1 concatenate.33
  15.5 0.7 concatenate.34.pos_ref
  16.2 15.1 %shard_map.104 = (f32[3,8192]{1,0:T(4,128)}, f32[32,2048]{1,0:T(8,128)}) custom-call(f32[8,8320]{1,0:T(8,128)} %concatenate.34.pos_ref, f32[3,8192]{1,0:T(4,128)} %nrm_ref.1, f32[1,8192]{1,0:T(1,128)} %bitcast.43, f32[6,8192]{1,0:T(8,128)} %wgt_ref.1, s32[6,8192]{1,0:T(8,128)} %add_select_fusion.con_ref, s32[1,8192]{1,0:T(1,128)} %bitcast.44, s32[1,8192]{1,0:T(1,128)} %bitcast.45), custom_call_target="tpu_custom_call" | custom-call | flops 3221225472 | bytes 40000000 | tf_op jit(solution)/shard_map/pallas_call | solution.py:262
  31.3 1.9 copy.13
  33.3 2.6 %all-to-all-start = ((f32[32,1,2048]{2,1,0:T(1,128)}), f32[32,1,2048]{2,1,0:T(1,128)S(1)}, u32[]{:S(2)}, u32[]{:S(2)}) async-start(f32[32,1,2048]{2,1,0:T(1,128)} %copy.13), calls=%async_computation | async-start | bytes 524288 | tf_op jit(solution)/shard_map/all_to_all | solution.py:351
  35.9 0.2 add_divide_fusion
  36.0 0.1 fusion.25
  36.1 3.6 %collective-permute-start.8 = (f32[16,32,128]{2,1,0:T(8,128)S(1)}, f32[16,32,128]{2,1,0:T(8,128)S(1)}, u32[]{:S(2)}, u32[]{:S(2)}) collective-permute-start(f32[16,32,128]{2,1,0:T(8,128)S(1)} %get-tuple-element.20), channel_id=1, source_target_pairs={{0,1},{1,2},{2,3},{4,5},{5,6},{6,7},{8,9},{9,10},{10,11},{12,13},{... | collective-permute-start | bytes 786440 | tf_op jit(solution)/shard_map/ppermute | solution.py:27
  39.7 1.3 collective-permute-start.9
  41.0 5.8 %all-to-all-done = f32[32,1,2048]{2,1,0:T(1,128)S(1)} async-done(((f32[32,1,2048]{2,1,0:T(1,128)}), f32[32,1,2048]{2,1,0:T(1,128)S(1)}, u32[]{:S(2)}, u32[]{:S(2)}) %all-to-all-start) | async-done | bytes 262176 | tf_op jit(solution)/shard_map/all_to_all | solution.py:351
  46.8 0.1 copy.18
  46.9 0.1 multiply_subtract_fusion
  47.0 0.8 copy.14.val_ref
  47.8 0.7 broadcast_in_dim.20.col_ref
  48.5 0.8 copy.15.row_ref
  49.3 46.5 %shard_map.105 = f32[512,512]{1,0:T(8,128)} custom-call(f32[512,512]{1,0:T(8,128)} %bitcast.42, f32[32,1,1024]{2,1,0:T(1,128)} %copy.14.val_ref, s32[32,1,1024]{2,1,0:T(1,128)} %copy.15.row_ref, s32[32,1,1024]{2,1,0:T(1,128)} %broadcast_in_dim.20.col_ref), custom_call_target="tpu_custom_call" | custom-call | flops 34359738368 | bytes 4000000 | tf_op jit(solution)/shard_map/pallas_call | solution.py:316
  95.7 1.2 fusion.26
  96.9 1.9 collective-permute-start.2
  98.8 1.3 collective-permute-start.3
  100.1 0.1 bitcast_reduce_fusion
  100.2 0.1 pad_maximum_fusion.17
  100.3 3.0 %collective-permute-start.10 = (f32[16,8,768]{2,1,0:T(8,128)S(1)}, f32[16,8,768]{2,1,0:T(8,128)S(1)}, u32[]{:S(2)}, u32[]{:S(2)}) collective-permute-start(f32[16,8,768]{2,1,0:T(8,128)S(1)} %get-tuple-element.14), channel_id=1, source_target_pairs={{0,4},{4,8},{8,12},{1,5},{5,9},{9,13},{2,6},{6,10},{10,14},{3,7},{... | collective-permute-start | bytes 1179656 | tf_op jit(solution)/shard_map/ppermute | solution.py:27
  103.3 1.3 collective-permute-start.11
  104.6 0.8 collective-permute-done.2
  105.4 4.1 %collective-permute-done.3 = f32[16,32,128]{2,1,0:T(8,128)S(1)} collective-permute-done((f32[16,32,128]{2,1,0:T(8,128)S(1)}, f32[16,32,128]{2,1,0:T(8,128)S(1)}, u32[]{:S(2)}, u32[]{:S(2)}) %collective-permute-start.3) | collective-permute-done | bytes 262176 | tf_op jit(solution)/shard_map/ppermute | solution.py:29
  109.5 0.1 pad_maximum_fusion.20
  109.6 1.3 collective-permute-start.4
  110.9 1.3 collective-permute-start.5
  112.2 11.4 %collective-permute-done.11 = f32[16,8,768]{2,1,0:T(8,128)S(1)} collective-permute-done((f32[16,8,768]{2,1,0:T(8,128)S(1)}, f32[16,8,768]{2,1,0:T(8,128)S(1)}, u32[]{:S(2)}, u32[]{:S(2)}) %collective-permute-start.11) | collective-permute-done | bytes 393248 | tf_op jit(solution)/shard_map/ppermute | solution.py:29
  123.6 0.1 pad_maximum_fusion.8
  123.7 1.3 collective-permute-start.12
  125.1 1.3 collective-permute-start.13
  126.4 11.6 %collective-permute-done.5 = f32[16,8,768]{2,1,0:T(8,128)S(1)} collective-permute-done((f32[16,8,768]{2,1,0:T(8,128)S(1)}, f32[16,8,768]{2,1,0:T(8,128)S(1)}, u32[]{:S(2)}, u32[]{:S(2)}) %collective-permute-start.5) | collective-permute-done | bytes 393248 | tf_op jit(solution)/shard_map/ppermute | solution.py:29
  138.0 0.1 pad_maximum_fusion.13
  138.1 1.3 collective-permute-start.6
  139.5 1.3 collective-permute-start.7
  140.8 0.4 fusion.2
  141.2 0.3 fusion.1
  141.5 2.1 pad_maximum_fusion.1.inverse
  143.7 2.2 pad_maximum_fusion.rhs
  145.8 15.4 %shard_map.106 = (f32[26,48,768]{2,1,0:T(8,128)}, f32[16,32,512]{2,1,0:T(8,128)}) custom-call(f32[26,48,768]{2,1,0:T(8,128)} %pad_maximum_fusion.rhs, f32[26,48,768]{2,1,0:T(8,128)} %pad_maximum_fusion.1.inverse, f32[16,32,512]{2,1,0:T(8,128)} %shift.1), custom_call_target="tpu_custom_call" | custom-call | tf_op jit(solution)/shard_map/pallas_call | solution.py:366
  161.2 1.4 bitcast_reduce_fusion.1
  162.5 0.4 fusion.3
  163.0 0.3 convolution_multiply_fusion.1
  163.3 4.3 %collective-permute-start.14 = (f32[2,8,16,128]{3,2,1,0:T(8,128)S(1)}, f32[2,8,16,128]{3,2,1,0:T(8,128)S(1)}, u32[]{:S(2)}, u32[]{:S(2)}) collective-permute-start(f32[2,8,16,128]{3,2,1,0:T(8,128)S(1)} %get-tuple-element.26), channel_id=1, source_target_pairs={{0,1},{1,2},{2,3},{4,5},{5,6},{6,7},{8,9},{9,10},{10,11},{12,13},{... | collective-permute-start | bytes 393224 | tf_op jit(solution)/shard_map/ppermute | solution.py:27
  167.6 1.3 collective-permute-start.15
  168.9 2.4 %collective-permute-done.14 = f32[2,8,16,128]{3,2,1,0:T(8,128)S(1)} collective-permute-done((f32[2,8,16,128]{3,2,1,0:T(8,128)S(1)}, f32[2,8,16,128]{3,2,1,0:T(8,128)S(1)}, u32[]{:S(2)}, u32[]{:S(2)}) %collective-permute-start.14) | collective-permute-done | bytes 131104 | tf_op jit(solution)/shard_map/ppermute | solution.py:27
  171.2 4.5 %collective-permute-done.15 = f32[2,8,16,128]{3,2,1,0:T(8,128)S(1)} collective-permute-done((f32[2,8,16,128]{3,2,1,0:T(8,128)S(1)}, f32[2,8,16,128]{3,2,1,0:T(8,128)S(1)}, u32[]{:S(2)}, u32[]{:S(2)}) %collective-permute-start.15) | collective-permute-done | bytes 131104 | tf_op jit(solution)/shard_map/ppermute | solution.py:29
  175.8 3.0 %collective-permute-start.16 = (f32[2,8,8,512]{3,2,1,0:T(8,128)S(1)}, f32[2,8,8,512]{3,2,1,0:T(8,128)S(1)}, u32[]{:S(2)}, u32[]{:S(2)}) collective-permute-start(f32[2,8,8,512]{3,2,1,0:T(8,128)S(1)} %get-tuple-element.24), channel_id=1, source_target_pairs={{0,4},{4,8},{8,12},{1,5},{5,9},{9,13},{2,6},{6,10},{10,14},{3,7},{... | collective-permute-start | bytes 786440 | tf_op jit(solution)/shard_map/ppermute | solution.py:27
  178.8 1.3 collective-permute-start.17
  180.1 4.4 %collective-permute-done.16 = f32[2,8,8,512]{3,2,1,0:T(8,128)S(1)} collective-permute-done((f32[2,8,8,512]{3,2,1,0:T(8,128)S(1)}, f32[2,8,8,512]{3,2,1,0:T(8,128)S(1)}, u32[]{:S(2)}, u32[]{:S(2)}) %collective-permute-start.16) | collective-permute-done | bytes 262176 | tf_op jit(solution)/shard_map/ppermute | solution.py:27
  184.5 6.4 %collective-permute-done.17 = f32[2,8,8,512]{3,2,1,0:T(8,128)S(1)} collective-permute-done((f32[2,8,8,512]{3,2,1,0:T(8,128)S(1)}, f32[2,8,8,512]{3,2,1,0:T(8,128)S(1)}, u32[]{:S(2)}, u32[]{:S(2)}) %collective-permute-start.17) | collective-permute-done | bytes 262176 | tf_op jit(solution)/shard_map/ppermute | solution.py:29
  190.9 0.1 pad_maximum_fusion.3
  191.0 0.2 fusion.24
  191.2 1.4 collective-permute-start.18
  192.6 1.5 collective-permute-start.19
  194.1 0.2 collective-permute-done.18
  194.2 2.3 %collective-permute-done.19 = f32[2,5,32,512]{3,2,1,0:T(8,128)S(1)} collective-permute-done((f32[2,5,32,512]{3,2,1,0:T(8,128)S(1)}, f32[2,5,32,512]{3,2,1,0:T(8,128)S(1)}, u32[]{:S(2)}, u32[]{:S(2)}) %collective-permute-start.19) | collective-permute-done | bytes 655392 | tf_op jit(solution)/shard_map/ppermute | solution.py:29
  196.6 1.7 pad_maximum_fusion.2.coarse
  198.3 21.9 %shard_map.107 = f32[16,32,512]{2,1,0:T(8,128)} custom-call(f32[2,18,32,512]{3,2,1,0:T(8,128)} %pad_maximum_fusion.2.coarse, f32[26,48,768]{2,1,0:T(8,128)} %pad_maximum_fusion.rhs, f32[26,48,768]{2,1,0:T(8,128)} %pad_maximum_fusion.1.inverse, f32[26,48,768]{2,1,0:T(8,128)} %get-tuple-element.8.smooth), custom_call_target="tpu_custom_call" | custom-call | tf_op jit(solution)/shard_map/pallas_call | solution.py:377
  (22 shorter events, 0.2 us)
Async XLA Ops:
  1.4 8.2 %collective-permute-start.1 = (f32[3,64]{1,0:T(4,128)S(1)}, f32[3,64]{1,0:T(4,128)S(1)}, u32[]{:S(2)}, u32[]{:S(2)}) collective-permute-start(f32[3,64]{1,0:T(4,128)S(1)} %get-tuple-element.30), channel_id=1, source_target_pairs={{1,0},{2,1},{3,2},{4,3},{5,4},{6,5},{7,6},{8,7},{9,8},{10,9},{11,1... | collective-permute-start | bytes 2312 | tf_op jit(solution)/shard_map/ppermute | solution.py:29
  7.8 6.6 %collective-permute-start = (f32[3,64]{1,0:T(4,128)S(1)}, f32[3,64]{1,0:T(4,128)S(1)}, u32[]{:S(2)}, u32[]{:S(2)}) collective-permute-start(f32[3,64]{1,0:T(4,128)S(1)} %get-tuple-element.31), channel_id=1, source_target_pairs={{0,1},{1,2},{2,3},{3,4},{4,5},{5,6},{6,7},{7,8},{8,9},{9,10},{10,1... | collective-permute-start | bytes 2312 | tf_op jit(solution)/shard_map/ppermute | solution.py:27
  16.2 19.6 %copy-start.1 = (f32[16,32,512]{2,1,0:T(8,128)S(1)}, f32[16,32,512]{2,1,0:T(8,128)}, u32[]{:S(2)}) copy-start(f32[16,32,512]{2,1,0:T(8,128)} %shift.1) | copy-start | bytes 3145732
  33.3 13.5 %all-to-all-start = ((f32[32,1,2048]{2,1,0:T(1,128)}), f32[32,1,2048]{2,1,0:T(1,128)S(1)}, u32[]{:S(2)}, u32[]{:S(2)}) async-start(f32[32,1,2048]{2,1,0:T(1,128)} %copy.13), calls=%async_computation | async-start | bytes 524288 | tf_op jit(solution)/shard_map/all_to_all | solution.py:351
  36.1 64.1 %collective-permute-start.8 = (f32[16,32,128]{2,1,0:T(8,128)S(1)}, f32[16,32,128]{2,1,0:T(8,128)S(1)}, u32[]{:S(2)}, u32[]{:S(2)}) collective-permute-start(f32[16,32,128]{2,1,0:T(8,128)S(1)} %get-tuple-element.20), channel_id=1, source_target_pairs={{0,1},{1,2},{2,3},{4,5},{5,6},{6,7},{8,9},{9,10},{10,11},{12,13},{... | collective-permute-start | bytes 786440 | tf_op jit(solution)/shard_map/ppermute | solution.py:27
  39.7 60.5 %collective-permute-start.9 = (f32[16,32,128]{2,1,0:T(8,128)S(1)}, f32[16,32,128]{2,1,0:T(8,128)S(1)}, u32[]{:S(2)}, u32[]{:S(2)}) collective-permute-start(f32[16,32,128]{2,1,0:T(8,128)S(1)} %get-tuple-element.21), channel_id=1, source_target_pairs={{1,0},{2,1},{3,2},{5,4},{6,5},{7,6},{9,8},{10,9},{11,10},{13,12},{... | collective-permute-start | bytes 786440 | tf_op jit(solution)/shard_map/ppermute | solution.py:29
  95.7 13.8 %copy-start = (f32[512,512]{1,0:T(8,128)S(1)}, f32[512,512]{1,0:T(8,128)}, u32[]{:S(2)}) copy-start(f32[512,512]{1,0:T(8,128)} %shard_map.105) | copy-start | bytes 3145732
  96.9 8.5 %collective-permute-start.2 = (f32[16,32,128]{2,1,0:T(8,128)S(1)}, f32[16,32,128]{2,1,0:T(8,128)S(1)}, u32[]{:S(2)}, u32[]{:S(2)}) collective-permute-start(f32[16,32,128]{2,1,0:T(8,128)S(1)} %get-tuple-element.22), channel_id=1, source_target_pairs={{0,1},{1,2},{2,3},{4,5},{5,6},{6,7},{8,9},{9,10},{10,11},{12,13},{... | collective-permute-start | bytes 786440 | tf_op jit(solution)/shard_map/ppermute | solution.py:27
  98.8 10.7 %collective-permute-start.3 = (f32[16,32,128]{2,1,0:T(8,128)S(1)}, f32[16,32,128]{2,1,0:T(8,128)S(1)}, u32[]{:S(2)}, u32[]{:S(2)}) collective-permute-start(f32[16,32,128]{2,1,0:T(8,128)S(1)} %get-tuple-element.23), channel_id=1, source_target_pairs={{1,0},{2,1},{3,2},{5,4},{6,5},{7,6},{9,8},{10,9},{11,10},{13,12},{... | collective-permute-start | bytes 786440 | tf_op jit(solution)/shard_map/ppermute | solution.py:29
  100.3 11.9 %collective-permute-start.10 = (f32[16,8,768]{2,1,0:T(8,128)S(1)}, f32[16,8,768]{2,1,0:T(8,128)S(1)}, u32[]{:S(2)}, u32[]{:S(2)}) collective-permute-start(f32[16,8,768]{2,1,0:T(8,128)S(1)} %get-tuple-element.14), channel_id=1, source_target_pairs={{0,4},{4,8},{8,12},{1,5},{5,9},{9,13},{2,6},{6,10},{10,14},{3,7},{... | collective-permute-start | bytes 1179656 | tf_op jit(solution)/shard_map/ppermute | solution.py:27
  103.3 20.3 %collective-permute-start.11 = (f32[16,8,768]{2,1,0:T(8,128)S(1)}, f32[16,8,768]{2,1,0:T(8,128)S(1)}, u32[]{:S(2)}, u32[]{:S(2)}) collective-permute-start(f32[16,8,768]{2,1,0:T(8,128)S(1)} %get-tuple-element.15), channel_id=1, source_target_pairs={{4,0},{8,4},{12,8},{5,1},{9,5},{13,9},{6,2},{10,6},{14,10},{7,3},{... | collective-permute-start | bytes 1179656 | tf_op jit(solution)/shard_map/ppermute | solution.py:29
  109.6 16.8 %collective-permute-start.4 = (f32[16,8,768]{2,1,0:T(8,128)S(1)}, f32[16,8,768]{2,1,0:T(8,128)S(1)}, u32[]{:S(2)}, u32[]{:S(2)}) collective-permute-start(f32[16,8,768]{2,1,0:T(8,128)S(1)} %get-tuple-element.16), channel_id=1, source_target_pairs={{0,4},{4,8},{8,12},{1,5},{5,9},{9,13},{2,6},{6,10},{10,14},{3,7},{... | collective-permute-start | bytes 1179656 | tf_op jit(solution)/shard_map/ppermute | solution.py:27
  110.9 27.1 %collective-permute-start.5 = (f32[16,8,768]{2,1,0:T(8,128)S(1)}, f32[16,8,768]{2,1,0:T(8,128)S(1)}, u32[]{:S(2)}, u32[]{:S(2)}) collective-permute-start(f32[16,8,768]{2,1,0:T(8,128)S(1)} %get-tuple-element.17), channel_id=1, source_target_pairs={{4,0},{8,4},{12,8},{5,1},{9,5},{13,9},{6,2},{10,6},{14,10},{7,3},{... | collective-permute-start | bytes 1179656 | tf_op jit(solution)/shard_map/ppermute | solution.py:29
  123.7 17.7 %collective-permute-start.12 = (f32[5,48,768]{2,1,0:T(8,128)S(1)}, f32[5,48,768]{2,1,0:T(8,128)S(1)}, u32[]{:S(2)}, u32[]{:S(2)}) collective-permute-start(f32[5,48,768]{2,1,0:T(8,128)S(1)} %get-tuple-element.10), channel_id=1, source_target_pairs={{0,16},{1,17},{2,18},{3,19},{4,20},{5,21},{6,22},{7,23},{8,24},{9,... | collective-permute-start | bytes 2211848 | tf_op jit(solution)/shard_map/ppermute | solution.py:27
  125.1 16.4 %collective-permute-start.13 = (f32[5,48,768]{2,1,0:T(8,128)S(1)}, f32[5,48,768]{2,1,0:T(8,128)S(1)}, u32[]{:S(2)}, u32[]{:S(2)}) collective-permute-start(f32[5,48,768]{2,1,0:T(8,128)S(1)} %get-tuple-element.11), channel_id=1, source_target_pairs={{16,0},{17,1},{18,2},{19,3},{20,4},{21,5},{22,6},{23,7},{24,8},{25... | collective-permute-start | bytes 2211848 | tf_op jit(solution)/shard_map/ppermute | solution.py:29
  138.1 5.5 %collective-permute-start.6 = (f32[5,48,768]{2,1,0:T(8,128)S(1)}, f32[5,48,768]{2,1,0:T(8,128)S(1)}, u32[]{:S(2)}, u32[]{:S(2)}) collective-permute-start(f32[5,48,768]{2,1,0:T(8,128)S(1)} %get-tuple-element.12), channel_id=1, source_target_pairs={{0,16},{1,17},{2,18},{3,19},{4,20},{5,21},{6,22},{7,23},{8,24},{9,... | collective-permute-start | bytes 2211848 | tf_op jit(solution)/shard_map/ppermute | solution.py:27
  139.5 4.2 %collective-permute-start.7 = (f32[5,48,768]{2,1,0:T(8,128)S(1)}, f32[5,48,768]{2,1,0:T(8,128)S(1)}, u32[]{:S(2)}, u32[]{:S(2)}) collective-permute-start(f32[5,48,768]{2,1,0:T(8,128)S(1)} %get-tuple-element.13), channel_id=1, source_target_pairs={{16,0},{17,1},{18,2},{19,3},{20,4},{21,5},{22,6},{23,7},{24,8},{25... | collective-permute-start | bytes 2211848 | tf_op jit(solution)/shard_map/ppermute | solution.py:29
  163.3 7.9 %collective-permute-start.14 = (f32[2,8,16,128]{3,2,1,0:T(8,128)S(1)}, f32[2,8,16,128]{3,2,1,0:T(8,128)S(1)}, u32[]{:S(2)}, u32[]{:S(2)}) collective-permute-start(f32[2,8,16,128]{3,2,1,0:T(8,128)S(1)} %get-tuple-element.26), channel_id=1, source_target_pairs={{0,1},{1,2},{2,3},{4,5},{5,6},{6,7},{8,9},{9,10},{10,11},{12,13},{... | collective-permute-start | bytes 393224 | tf_op jit(solution)/shard_map/ppermute | solution.py:27
  167.6 8.2 %collective-permute-start.15 = (f32[2,8,16,128]{3,2,1,0:T(8,128)S(1)}, f32[2,8,16,128]{3,2,1,0:T(8,128)S(1)}, u32[]{:S(2)}, u32[]{:S(2)}) collective-permute-start(f32[2,8,16,128]{3,2,1,0:T(8,128)S(1)} %get-tuple-element.27), channel_id=1, source_target_pairs={{1,0},{2,1},{3,2},{5,4},{6,5},{7,6},{9,8},{10,9},{11,10},{13,12},{... | collective-permute-start | bytes 393224 | tf_op jit(solution)/shard_map/ppermute | solution.py:29
  175.8 8.7 %collective-permute-start.16 = (f32[2,8,8,512]{3,2,1,0:T(8,128)S(1)}, f32[2,8,8,512]{3,2,1,0:T(8,128)S(1)}, u32[]{:S(2)}, u32[]{:S(2)}) collective-permute-start(f32[2,8,8,512]{3,2,1,0:T(8,128)S(1)} %get-tuple-element.24), channel_id=1, source_target_pairs={{0,4},{4,8},{8,12},{1,5},{5,9},{9,13},{2,6},{6,10},{10,14},{3,7},{... | collective-permute-start | bytes 786440 | tf_op jit(solution)/shard_map/ppermute | solution.py:27
  178.8 12.1 %collective-permute-start.17 = (f32[2,8,8,512]{3,2,1,0:T(8,128)S(1)}, f32[2,8,8,512]{3,2,1,0:T(8,128)S(1)}, u32[]{:S(2)}, u32[]{:S(2)}) collective-permute-start(f32[2,8,8,512]{3,2,1,0:T(8,128)S(1)} %get-tuple-element.25), channel_id=1, source_target_pairs={{4,0},{8,4},{12,8},{5,1},{9,5},{13,9},{6,2},{10,6},{14,10},{7,3},{... | collective-permute-start | bytes 786440 | tf_op jit(solution)/shard_map/ppermute | solution.py:29
  191.2 3.1 %collective-permute-start.18 = (f32[2,5,32,512]{3,2,1,0:T(8,128)S(1)}, f32[2,5,32,512]{3,2,1,0:T(8,128)S(1)}, u32[]{:S(2)}, u32[]{:S(2)}) collective-permute-start(f32[2,5,32,512]{3,2,1,0:T(8,128)S(1)} %get-tuple-element.18), channel_id=1, source_target_pairs={{0,16},{1,17},{2,18},{3,19},{4,20},{5,21},{6,22},{7,23},{8,24},{9,... | collective-permute-start | bytes 1966088 | tf_op jit(solution)/shard_map/ppermute | solution.py:27
  192.6 4.0 %collective-permute-start.19 = (f32[2,5,32,512]{3,2,1,0:T(8,128)S(1)}, f32[2,5,32,512]{3,2,1,0:T(8,128)S(1)}, u32[]{:S(2)}, u32[]{:S(2)}) collective-permute-start(f32[2,5,32,512]{3,2,1,0:T(8,128)S(1)} %get-tuple-element.19), channel_id=1, source_target_pairs={{16,0},{17,1},{18,2},{19,3},{20,4},{21,5},{22,6},{23,7},{24,8},{25... | collective-permute-start | bytes 1966088 | tf_op jit(solution)/shard_map/ppermute | solution.py:29

commit v3 on v2

--- a/solution.py
+++ b/solution.py
@@ -348,16 +348,21 @@
         padded, normals, tension, edge_weight, relative, owner_map[:, 0], cell_map,
         ndevice, capacity,
     )
+    wx, wy, wz = 2 * SMOOTH - 1, 8, 128
+    sides = (("gz", 2, wz), ("gy", 1, wy), ("gx", 0, wx))
+    inverse = padded_2(1.0 / (6.0 + shift_diag), sides[:1], False)
+    packed, inverse = lax.optimization_barrier((packed, inverse))
+    inverse = padded_2(inverse, sides[1:2], False)
     got = lax.all_to_all(packed, ("gx", "gy", "gz"), split_axis=0, concat_axis=0, tiled=True)
+    got, inverse = lax.optimization_barrier((got, inverse))
+    inverse = padded_2(inverse, sides[2:], False)
     forcing = scatter(pressure_rhs, got[:, :capacity], got[:, capacity:].astype(jnp.int32))
 
     nx, ny, nz = pressure_rhs.shape
-    wx, wy, wz = 2 * SMOOTH - 1, 8, 128
     cx = COARSE_SMOOTH - 1 + (SMOOTH + 1) // 2
-    sides = (("gz", 2, wz), ("gy", 1, wy), ("gx", 0, wx))
     coarse_sides = (("gz", 3, wz), ("gy", 2, wy), ("gx", 1, cx))
     coarse_shift = 0.5 * pool(shift_diag)
-    inverse = padded_2(1.0 / (6.0 + shift_diag), sides, False)
+    forcing, inverse = lax.optimization_barrier((forcing, inverse))
     rhs = padded_2(forcing, sides, False)
     wide = jax.ShapeDtypeStruct(rhs.shape, jnp.float32)
     core = jax.ShapeDtypeStruct(pressure_rhs.shape, jnp.float32)

time: 221 us -> 232 us (1.050)
  starting transfers between devices: 41.9 us -> 51.4 us
  other arithmetic: 9.97 us -> 13 us
    all_to_all x1, starting transfers between devices: 2.59 us -> 10.6 us  [body(): lax.all_to_all(packed, ('gx', 'gy', 'gz'), split_axis=0, concat_axis=0, t...]
    ppermute x10, waiting for transfers between devices: 12.6 us -> 19.4 us  [padded_2(): lax.ppermute(tail, axis, [(i, (i + 1) % count) for i in range(ends)])]
    all_to_all x1, waiting for transfers between devices: 5.78 us -> 1.2 us  [body(): lax.all_to_all(packed, ('gx', 'gy', 'gz'), split_axis=0, concat_axis=0, t...]
    ppermute x10, waiting for transfers between devices: 40.4 us -> 36.7 us  [padded_2(): lax.ppermute(head, axis, [((i + 1) % count, i) for i in range(ends)])]
    concatenate x5 -> x7, other arithmetic: 6.16 us -> 9.12 us  [padded_2(): jnp.concatenate([lax.ppermute(tail, axis, [(i, (i + 1) % count) for i in...]
  transfers between devices with their start and end apart: 21 -> 21, of which waited for: 12 -> 14; matrix products, arithmetic and copies ran while one was open for 4% -> 3% of each run, Pallas kernels for 21% -> 27%
where the time goes in v3:
time: 232 us; the launch traced here: 231 us
  Pallas kernels  98.8 us (43%)
  waiting for transfers between devices  57.2 us (25%)
  starting transfers between devices  51.4 us (22%)
  other arithmetic  13 us (6%)
  local copies, waits for them, and re-layouts  8.08 us (3%)
    pallas_call x1, Pallas kernels, scatter(): pl.pallas_call(scatter_kernel, grid=(sources,), in_specs=[whole, one, one...  46.5 us
    ppermute x10, waiting for transfers between devices, padded_2(): lax.ppermute(head, axis, [((i + 1) % count, i) for i in range(ends)])  36.7 us
    ppermute x10, starting transfers between devices, padded_2(): lax.ppermute(tail, axis, [(i, (i + 1) % count) for i in range(ends)])  22.6 us
    pallas_call x1, Pallas kernels, body(): pl.pallas_call(functools.partial(up_kernel, wx, wy, wz, cx), in_specs=[vm...  21.9 us
    ppermute x10, waiting for transfers between devices, padded_2(): lax.ppermute(tail, axis, [(i, (i + 1) % count) for i in range(ends)])  19.4 us
    ppermute x10, starting transfers between devices, padded_2(): lax.ppermute(head, axis, [((i + 1) % count, i) for i in range(ends)])  18.2 us
    pallas_call x1, Pallas kernels, body(): pl.pallas_call(functools.partial(down_kernel, wx, wy, wz), in_specs=[vmem...  15.4 us
    pallas_call x1, Pallas kernels, points(): pl.pallas_call(functools.partial(points_kernel, ndevice, capacity), grid=...  15 us
  transfers between devices with their start and end apart: 21, of which 14 were waited for; matrix products, arithmetic and copies ran while one was open for 3% of the time, Pallas kernels for 27%

profile of v3, /device:TPU:0, one launch (start us, length us, event | category | flops | bytes accessed | tf_op | source)
XLA Modules:
  0.0 231.0 jit_solution(12196089294003720015)
XLA Ops:
  0.6 0.8 fusion.31
  1.5 6.4 %collective-permute-start.1 = (f32[3,64]{1,0:T(4,128)S(1)}, f32[3,64]{1,0:T(4,128)S(1)}, u32[]{:S(2)}, u32[]{:S(2)}) collective-permute-start(f32[3,64]{1,0:T(4,128)S(1)} %get-tuple-element.42), channel_id=1, source_target_pairs={{1,0},{2,1},{3,2},{4,3},{5,4},{6,5},{7,6},{8,7},{9,8},{10,9},{11,1... | collective-permute-start | bytes 2312 | tf_op jit(solution)/shard_map/ppermute | solution.py:29
  7.9 1.4 add_divide_fusion
  9.3 1.3 collective-permute-start.2
  10.6 1.3 collective-permute-start.3
  12.0 0.8 add_select_fusion.con_ref
  12.8 1.7 collective-permute-done
  14.5 0.2 concatenate.33
  14.7 0.7 concatenate.34.pos_ref
  15.4 15.0 %shard_map.104 = (f32[3,8192]{1,0:T(4,128)}, f32[32,2048]{1,0:T(8,128)}) custom-call(f32[8,8320]{1,0:T(8,128)} %concatenate.34.pos_ref, f32[3,8192]{1,0:T(4,128)} %nrm_ref.1, f32[1,8192]{1,0:T(1,128)} %bitcast.41, f32[6,8192]{1,0:T(8,128)} %wgt_ref.1, s32[6,8192]{1,0:T(8,128)} %add_select_fusion.con_ref, s32[1,8192]{1,0:T(1,128)} %bitcast.42, s32[1,8192]{1,0:T(1,128)} %bitcast.43), custom_call_target="tpu_custom_call" | custom-call | flops 3221225472 | bytes 40000000 | tf_op jit(solution)/shard_map/pallas_call | solution.py:262
  30.5 0.1 pad_maximum_fusion.4
  30.6 1.2 copy-done
  31.9 1.7 collective-permute-start.4
  33.6 1.3 collective-permute-start.5
  34.9 1.0 copy.13
  35.9 10.6 %all-to-all-start = ((f32[32,1,2048]{2,1,0:T(1,128)}), f32[32,1,2048]{2,1,0:T(1,128)S(1)}, u32[]{:S(2)}, u32[]{:S(2)}) async-start(f32[32,1,2048]{2,1,0:T(1,128)} %copy.13), calls=%async_computation | async-start | bytes 524288 | tf_op jit(solution)/shard_map/all_to_all | solution.py:356
  46.5 8.1 %collective-permute-done.5 = f32[16,8,768]{2,1,0:T(8,128)S(1)} collective-permute-done((f32[16,8,768]{2,1,0:T(8,128)S(1)}, f32[16,8,768]{2,1,0:T(8,128)S(1)}, u32[]{:S(2)}, u32[]{:S(2)}) %collective-permute-start.5) | collective-permute-done | bytes 393248 | tf_op jit(solution)/shard_map/ppermute | solution.py:29
  54.6 1.6 pad_maximum_fusion.2
  56.3 1.2 all-to-all-done
  57.6 0.1 multiply_subtract_fusion
  57.7 0.8 copy.14.val_ref
  58.5 0.7 broadcast_in_dim.20.col_ref
  59.2 0.8 copy.15.row_ref
  60.0 1.3 fusion.24
  61.2 1.3 collective-permute-start.6
  62.6 1.3 collective-permute-start.7
  63.9 46.5 %shard_map.105 = f32[512,512]{1,0:T(8,128)} custom-call(f32[512,512]{1,0:T(8,128)} %bitcast.40, f32[32,1,1024]{2,1,0:T(1,128)} %copy.14.val_ref, s32[32,1,1024]{2,1,0:T(1,128)} %copy.15.row_ref, s32[32,1,1024]{2,1,0:T(1,128)} %broadcast_in_dim.20.col_ref), custom_call_target="tpu_custom_call" | custom-call | flops 34359738368 | bytes 4000000 | tf_op jit(solution)/shard_map/pallas_call | solution.py:316
  110.4 3.3 %pad_maximum_fusion.inverse = f32[26,48,768]{2,1,0:T(8,128)} fusion(f32[5,48,768]{2,1,0:T(8,128)} %collective-permute-done.7, f32[16,48,768]{2,1,0:T(8,128)S(1)} %pad_maximum_fusion.2, f32[5,48,768]{2,1,0:T(8,128)S(1)} %collective-permute-done.6), kind=kLoop, calls=%fused_computation | loop fusion | flops 1916928 | bytes 7667712 | tf_op jit(solution)/shard_map/concatenate | solution.py:25
  113.7 3.2 %collective-permute-start.8 = (f32[16,32,128]{2,1,0:T(8,128)S(1)}, f32[16,32,128]{2,1,0:T(8,128)S(1)}, u32[]{:S(2)}, u32[]{:S(2)}) collective-permute-start(f32[16,32,128]{2,1,0:T(8,128)S(1)} %get-tuple-element.33), channel_id=1, source_target_pairs={{0,1},{1,2},{2,3},{4,5},{5,6},{6,7},{8,9},{9,10},{10,11},{12,13},{... | collective-permute-start | bytes 786440 | tf_op jit(solution)/shard_map/ppermute | solution.py:27
  116.9 1.3 collective-permute-start.9
  118.2 4.3 %collective-permute-done.8 = f32[16,32,128]{2,1,0:T(8,128)S(1)} collective-permute-done((f32[16,32,128]{2,1,0:T(8,128)S(1)}, f32[16,32,128]{2,1,0:T(8,128)S(1)}, u32[]{:S(2)}, u32[]{:S(2)}) %collective-permute-start.8) | collective-permute-done | bytes 262176 | tf_op jit(solution)/shard_map/ppermute | solution.py:27
  122.6 4.9 %collective-permute-done.9 = f32[16,32,128]{2,1,0:T(8,128)S(1)} collective-permute-done((f32[16,32,128]{2,1,0:T(8,128)S(1)}, f32[16,32,128]{2,1,0:T(8,128)S(1)}, u32[]{:S(2)}, u32[]{:S(2)}) %collective-permute-start.9) | collective-permute-done | bytes 262176 | tf_op jit(solution)/shard_map/ppermute | solution.py:29
  127.6 5.0 %collective-permute-start.10 = (f32[16,8,768]{2,1,0:T(8,128)S(1)}, f32[16,8,768]{2,1,0:T(8,128)S(1)}, u32[]{:S(2)}, u32[]{:S(2)}) collective-permute-start(f32[16,8,768]{2,1,0:T(8,128)S(1)} %get-tuple-element.26), channel_id=1, source_target_pairs={{0,4},{4,8},{8,12},{1,5},{5,9},{9,13},{2,6},{6,10},{10,14},{3,7},{... | collective-permute-start | bytes 1179656 | tf_op jit(solution)/shard_map/ppermute | solution.py:27
  132.7 1.3 collective-permute-start.11
  134.0 8.0 %collective-permute-done.10 = f32[16,8,768]{2,1,0:T(8,128)S(1)} collective-permute-done((f32[16,8,768]{2,1,0:T(8,128)S(1)}, f32[16,8,768]{2,1,0:T(8,128)S(1)}, u32[]{:S(2)}, u32[]{:S(2)}) %collective-permute-start.10) | collective-permute-done | bytes 393248 | tf_op jit(solution)/shard_map/ppermute | solution.py:27
  142.0 8.9 %collective-permute-done.11 = f32[16,8,768]{2,1,0:T(8,128)S(1)} collective-permute-done((f32[16,8,768]{2,1,0:T(8,128)S(1)}, f32[16,8,768]{2,1,0:T(8,128)S(1)}, u32[]{:S(2)}, u32[]{:S(2)}) %collective-permute-start.11) | collective-permute-done | bytes 393248 | tf_op jit(solution)/shard_map/ppermute | solution.py:29
  150.9 0.1 pad_maximum_fusion.8
  151.0 2.1 collective-permute-start.12
  153.1 1.3 collective-permute-start.13
  154.4 0.1 bitcast_reduce_fusion
  154.5 0.4 fusion.2
  154.9 0.3 fusion.1
  155.2 2.0 collective-permute-done.13
  157.2 2.2 pad_maximum_fusion.1.rhs
  159.4 15.4 %shard_map.106 = (f32[26,48,768]{2,1,0:T(8,128)}, f32[16,32,512]{2,1,0:T(8,128)}) custom-call(f32[26,48,768]{2,1,0:T(8,128)} %pad_maximum_fusion.1.rhs, f32[26,48,768]{2,1,0:T(8,128)} %pad_maximum_fusion.inverse, f32[16,32,512]{2,1,0:T(8,128)} %shift.1), custom_call_target="tpu_custom_call" | custom-call | tf_op jit(solution)/shard_map/pallas_call | solution.py:371
  174.7 1.4 bitcast_reduce_fusion.1
  176.1 0.4 fusion.3
  176.5 0.3 convolution_multiply_fusion.1
  176.8 4.1 %collective-permute-start.14 = (f32[2,8,16,128]{3,2,1,0:T(8,128)S(1)}, f32[2,8,16,128]{3,2,1,0:T(8,128)S(1)}, u32[]{:S(2)}, u32[]{:S(2)}) collective-permute-start(f32[2,8,16,128]{3,2,1,0:T(8,128)S(1)} %get-tuple-element.38), channel_id=1, source_target_pairs={{0,1},{1,2},{2,3},{4,5},{5,6},{6,7},{8,9},{9,10},{10,11},{12,13},{... | collective-permute-start | bytes 393224 | tf_op jit(solution)/shard_map/ppermute | solution.py:27
  180.9 1.3 collective-permute-start.15
  182.2 1.7 collective-permute-done.14
  183.9 4.1 %collective-permute-done.15 = f32[2,8,16,128]{3,2,1,0:T(8,128)S(1)} collective-permute-done((f32[2,8,16,128]{3,2,1,0:T(8,128)S(1)}, f32[2,8,16,128]{3,2,1,0:T(8,128)S(1)}, u32[]{:S(2)}, u32[]{:S(2)}) %collective-permute-start.15) | collective-permute-done | bytes 131104 | tf_op jit(solution)/shard_map/ppermute | solution.py:29
  188.1 2.5 %collective-permute-start.16 = (f32[2,8,8,512]{3,2,1,0:T(8,128)S(1)}, f32[2,8,8,512]{3,2,1,0:T(8,128)S(1)}, u32[]{:S(2)}, u32[]{:S(2)}) collective-permute-start(f32[2,8,8,512]{3,2,1,0:T(8,128)S(1)} %get-tuple-element.36), channel_id=1, source_target_pairs={{0,4},{4,8},{8,12},{1,5},{5,9},{9,13},{2,6},{6,10},{10,14},{3,7},{... | collective-permute-start | bytes 786440 | tf_op jit(solution)/shard_map/ppermute | solution.py:27
  190.7 1.3 collective-permute-start.17
  192.0 3.4 %collective-permute-done.16 = f32[2,8,8,512]{3,2,1,0:T(8,128)S(1)} collective-permute-done((f32[2,8,8,512]{3,2,1,0:T(8,128)S(1)}, f32[2,8,8,512]{3,2,1,0:T(8,128)S(1)}, u32[]{:S(2)}, u32[]{:S(2)}) %collective-permute-start.16) | collective-permute-done | bytes 262176 | tf_op jit(solution)/shard_map/ppermute | solution.py:27
  195.4 6.4 %collective-permute-done.17 = f32[2,8,8,512]{3,2,1,0:T(8,128)S(1)} collective-permute-done((f32[2,8,8,512]{3,2,1,0:T(8,128)S(1)}, f32[2,8,8,512]{3,2,1,0:T(8,128)S(1)}, u32[]{:S(2)}, u32[]{:S(2)}) %collective-permute-start.17) | collective-permute-done | bytes 262176 | tf_op jit(solution)/shard_map/ppermute | solution.py:29
  201.7 0.1 pad_maximum_fusion.5
  201.9 0.2 fusion.27
  202.0 1.3 collective-permute-start.18
  203.4 1.5 collective-permute-start.19
  204.8 0.2 collective-permute-done.18
  205.0 2.3 %collective-permute-done.19 = f32[2,5,32,512]{3,2,1,0:T(8,128)S(1)} collective-permute-done((f32[2,5,32,512]{3,2,1,0:T(8,128)S(1)}, f32[2,5,32,512]{3,2,1,0:T(8,128)S(1)}, u32[]{:S(2)}, u32[]{:S(2)}) %collective-permute-start.19) | collective-permute-done | bytes 655392 | tf_op jit(solution)/shard_map/ppermute | solution.py:29
  207.4 1.7 pad_maximum_fusion.3.coarse
  209.1 21.9 %shard_map.107 = f32[16,32,512]{2,1,0:T(8,128)} custom-call(f32[2,18,32,512]{3,2,1,0:T(8,128)} %pad_maximum_fusion.3.coarse, f32[26,48,768]{2,1,0:T(8,128)} %pad_maximum_fusion.1.rhs, f32[26,48,768]{2,1,0:T(8,128)} %pad_maximum_fusion.inverse, f32[26,48,768]{2,1,0:T(8,128)} %get-tuple-element.20.smooth), custom_call_target="tpu_custom_call" | custom-call | tf_op jit(solution)/shard_map/pallas_call | solution.py:382
  (35 shorter events, 0.6 us)
Async XLA Ops:
  0.6 13.8 %copy-start.5 = (f32[3,8192]{1,0:T(4,128)S(1)}, f32[3,8192]{1,0:T(4,128)}, u32[]{:S(2)}) copy-start(f32[3,8192]{1,0:T(4,128)} %param.11) | copy-start | bytes 294916
  0.6 11.3 %copy-start.3 = (s32[6,8192]{1,0:T(8,128)S(1)}, s32[6,8192]{1,0:T(8,128)}, u32[]{:S(2)}) copy-start(s32[6,8192]{1,0:T(8,128)} %param.17) | copy-start | bytes 589828
  1.5 11.3 %collective-permute-start.1 = (f32[3,64]{1,0:T(4,128)S(1)}, f32[3,64]{1,0:T(4,128)S(1)}, u32[]{:S(2)}, u32[]{:S(2)}) collective-permute-start(f32[3,64]{1,0:T(4,128)S(1)} %get-tuple-element.42), channel_id=1, source_target_pairs={{1,0},{2,1},{3,2},{4,3},{5,4},{6,5},{7,6},{8,7},{9,8},{10,9},{11,1... | collective-permute-start | bytes 2312 | tf_op jit(solution)/shard_map/ppermute | solution.py:29
  7.9 6.6 %collective-permute-start = (f32[3,64]{1,0:T(4,128)S(1)}, f32[3,64]{1,0:T(4,128)S(1)}, u32[]{:S(2)}, u32[]{:S(2)}) collective-permute-start(f32[3,64]{1,0:T(4,128)S(1)} %get-tuple-element.43), channel_id=1, source_target_pairs={{0,1},{1,2},{2,3},{3,4},{4,5},{5,6},{6,7},{7,8},{8,9},{9,10},{10,1... | collective-permute-start | bytes 2312 | tf_op jit(solution)/shard_map/ppermute | solution.py:27
  9.3 21.1 %collective-permute-start.2 = (f32[16,32,128]{2,1,0:T(8,128)S(1)}, f32[16,32,128]{2,1,0:T(8,128)S(1)}, u32[]{:S(2)}, u32[]{:S(2)}) collective-permute-start(f32[16,32,128]{2,1,0:T(8,128)S(1)} %get-tuple-element.34), channel_id=1, source_target_pairs={{0,1},{1,2},{2,3},{4,5},{5,6},{6,7},{8,9},{9,10},{10,11},{12,13},{... | collective-permute-start | bytes 786440 | tf_op jit(solution)/shard_map/ppermute | solution.py:27
  10.6 19.8 %collective-permute-start.3 = (f32[16,32,128]{2,1,0:T(8,128)S(1)}, f32[16,32,128]{2,1,0:T(8,128)S(1)}, u32[]{:S(2)}, u32[]{:S(2)}) collective-permute-start(f32[16,32,128]{2,1,0:T(8,128)S(1)} %get-tuple-element.35), channel_id=1, source_target_pairs={{1,0},{2,1},{3,2},{5,4},{6,5},{7,6},{9,8},{10,9},{11,10},{13,12},{... | collective-permute-start | bytes 786440 | tf_op jit(solution)/shard_map/ppermute | solution.py:29
  30.5 4.4 %copy-start.4 = (f32[32,2048]{1,0:T(8,128)S(1)}, f32[32,2048]{1,0:T(8,128)}, u32[]{:S(2)}) copy-start(f32[32,2048]{1,0:T(8,128)} %get-tuple-element.13) | copy-start | bytes 786436
  30.6 1.2 copy-start
  31.9 14.7 %collective-permute-start.4 = (f32[16,8,768]{2,1,0:T(8,128)S(1)}, f32[16,8,768]{2,1,0:T(8,128)S(1)}, u32[]{:S(2)}, u32[]{:S(2)}) collective-permute-start(f32[16,8,768]{2,1,0:T(8,128)S(1)} %get-tuple-element.28), channel_id=1, source_target_pairs={{0,4},{4,8},{8,12},{1,5},{5,9},{9,13},{2,6},{6,10},{10,14},{3,7},{... | collective-permute-start | bytes 1179656 | tf_op jit(solution)/shard_map/ppermute | solution.py:27
  33.6 21.0 %collective-permute-start.5 = (f32[16,8,768]{2,1,0:T(8,128)S(1)}, f32[16,8,768]{2,1,0:T(8,128)S(1)}, u32[]{:S(2)}, u32[]{:S(2)}) collective-permute-start(f32[16,8,768]{2,1,0:T(8,128)S(1)} %get-tuple-element.29), channel_id=1, source_target_pairs={{4,0},{8,4},{12,8},{5,1},{9,5},{13,9},{6,2},{10,6},{14,10},{7,3},{... | collective-permute-start | bytes 1179656 | tf_op jit(solution)/shard_map/ppermute | solution.py:29
  35.9 21.6 %all-to-all-start = ((f32[32,1,2048]{2,1,0:T(1,128)}), f32[32,1,2048]{2,1,0:T(1,128)S(1)}, u32[]{:S(2)}, u32[]{:S(2)}) async-start(f32[32,1,2048]{2,1,0:T(1,128)} %copy.13), calls=%async_computation | async-start | bytes 524288 | tf_op jit(solution)/shard_map/all_to_all | solution.py:356
  61.2 49.1 %collective-permute-start.6 = (f32[5,48,768]{2,1,0:T(8,128)}, f32[5,48,768]{2,1,0:T(8,128)S(1)}, u32[]{:S(2)}, u32[]{:S(2)}) collective-permute-start(f32[5,48,768]{2,1,0:T(8,128)} %get-tuple-element.24), channel_id=1, source_target_pairs={{0,16},{1,17},{2,18},{3,19},{4,20},{5,21},{6,22},{7,23},{8,24},{9,... | collective-permute-start | bytes 2211848 | tf_op jit(solution)/shard_map/ppermute | solution.py:27
  62.6 47.8 %collective-permute-start.7 = (f32[5,48,768]{2,1,0:T(8,128)}, f32[5,48,768]{2,1,0:T(8,128)}, u32[]{:S(2)}, u32[]{:S(2)}) collective-permute-start(f32[5,48,768]{2,1,0:T(8,128)} %get-tuple-element.25), channel_id=1, source_target_pairs={{16,0},{17,1},{18,2},{19,3},{20,4},{21,5},{22,6},{23,7},{24,8},{25... | collective-permute-start | bytes 2211848 | tf_op jit(solution)/shard_map/ppermute | solution.py:29
  110.3 3.3 %copy-start.2 = (f32[512,512]{1,0:T(8,128)S(1)}, f32[512,512]{1,0:T(8,128)}, u32[]{:S(2)}) copy-start(f32[512,512]{1,0:T(8,128)} %shard_map.105) | copy-start | bytes 3145732
  113.7 8.8 %collective-permute-start.8 = (f32[16,32,128]{2,1,0:T(8,128)S(1)}, f32[16,32,128]{2,1,0:T(8,128)S(1)}, u32[]{:S(2)}, u32[]{:S(2)}) collective-permute-start(f32[16,32,128]{2,1,0:T(8,128)S(1)} %get-tuple-element.33), channel_id=1, source_target_pairs={{0,1},{1,2},{2,3},{4,5},{5,6},{6,7},{8,9},{9,10},{10,11},{12,13},{... | collective-permute-start | bytes 786440 | tf_op jit(solution)/shard_map/ppermute | solution.py:27
  116.9 10.7 %collective-permute-start.9 = (f32[16,32,128]{2,1,0:T(8,128)S(1)}, f32[16,32,128]{2,1,0:T(8,128)S(1)}, u32[]{:S(2)}, u32[]{:S(2)}) collective-permute-start(f32[16,32,128]{2,1,0:T(8,128)S(1)} %get-tuple-element.32), channel_id=1, source_target_pairs={{1,0},{2,1},{3,2},{5,4},{6,5},{7,6},{9,8},{10,9},{11,10},{13,12},{... | collective-permute-start | bytes 786440 | tf_op jit(solution)/shard_map/ppermute | solution.py:29
  127.6 26.8 %copy-start.1 = (f32[16,32,512]{2,1,0:T(8,128)S(1)}, f32[16,32,512]{2,1,0:T(8,128)}, u32[]{:S(2)}) copy-start(f32[16,32,512]{2,1,0:T(8,128)} %shift.1) | copy-start | bytes 3145732
  127.6 14.3 %collective-permute-start.10 = (f32[16,8,768]{2,1,0:T(8,128)S(1)}, f32[16,8,768]{2,1,0:T(8,128)S(1)}, u32[]{:S(2)}, u32[]{:S(2)}) collective-permute-start(f32[16,8,768]{2,1,0:T(8,128)S(1)} %get-tuple-element.26), channel_id=1, source_target_pairs={{0,4},{4,8},{8,12},{1,5},{5,9},{9,13},{2,6},{6,10},{10,14},{3,7},{... | collective-permute-start | bytes 1179656 | tf_op jit(solution)/shard_map/ppermute | solution.py:27
  132.7 18.2 %collective-permute-start.11 = (f32[16,8,768]{2,1,0:T(8,128)S(1)}, f32[16,8,768]{2,1,0:T(8,128)S(1)}, u32[]{:S(2)}, u32[]{:S(2)}) collective-permute-start(f32[16,8,768]{2,1,0:T(8,128)S(1)} %get-tuple-element.27), channel_id=1, source_target_pairs={{4,0},{8,4},{12,8},{5,1},{9,5},{13,9},{6,2},{10,6},{14,10},{7,3},{... | collective-permute-start | bytes 1179656 | tf_op jit(solution)/shard_map/ppermute | solution.py:29
  151.0 4.2 %collective-permute-start.12 = (f32[5,48,768]{2,1,0:T(8,128)S(1)}, f32[5,48,768]{2,1,0:T(8,128)S(1)}, u32[]{:S(2)}, u32[]{:S(2)}) collective-permute-start(f32[5,48,768]{2,1,0:T(8,128)S(1)} %get-tuple-element.22), channel_id=1, source_target_pairs={{0,16},{1,17},{2,18},{3,19},{4,20},{5,21},{6,22},{7,23},{8,24},{9,... | collective-permute-start | bytes 2211848 | tf_op jit(solution)/shard_map/ppermute | solution.py:27
  153.1 4.1 %collective-permute-start.13 = (f32[5,48,768]{2,1,0:T(8,128)S(1)}, f32[5,48,768]{2,1,0:T(8,128)S(1)}, u32[]{:S(2)}, u32[]{:S(2)}) collective-permute-start(f32[5,48,768]{2,1,0:T(8,128)S(1)} %get-tuple-element.23), channel_id=1, source_target_pairs={{16,0},{17,1},{18,2},{19,3},{20,4},{21,5},{22,6},{23,7},{24,8},{25... | collective-permute-start | bytes 2211848 | tf_op jit(solution)/shard_map/ppermute | solution.py:29
  176.8 7.1 %collective-permute-start.14 = (f32[2,8,16,128]{3,2,1,0:T(8,128)S(1)}, f32[2,8,16,128]{3,2,1,0:T(8,128)S(1)}, u32[]{:S(2)}, u32[]{:S(2)}) collective-permute-start(f32[2,8,16,128]{3,2,1,0:T(8,128)S(1)} %get-tuple-element.38), channel_id=1, source_target_pairs={{0,1},{1,2},{2,3},{4,5},{5,6},{6,7},{8,9},{9,10},{10,11},{12,13},{... | collective-permute-start | bytes 393224 | tf_op jit(solution)/shard_map/ppermute | solution.py:27
  180.9 7.2 %collective-permute-start.15 = (f32[2,8,16,128]{3,2,1,0:T(8,128)S(1)}, f32[2,8,16,128]{3,2,1,0:T(8,128)S(1)}, u32[]{:S(2)}, u32[]{:S(2)}) collective-permute-start(f32[2,8,16,128]{3,2,1,0:T(8,128)S(1)} %get-tuple-element.39), channel_id=1, source_target_pairs={{1,0},{2,1},{3,2},{5,4},{6,5},{7,6},{9,8},{10,9},{11,10},{13,12},{... | collective-permute-start | bytes 393224 | tf_op jit(solution)/shard_map/ppermute | solution.py:29
  188.1 7.2 %collective-permute-start.16 = (f32[2,8,8,512]{3,2,1,0:T(8,128)S(1)}, f32[2,8,8,512]{3,2,1,0:T(8,128)S(1)}, u32[]{:S(2)}, u32[]{:S(2)}) collective-permute-start(f32[2,8,8,512]{3,2,1,0:T(8,128)S(1)} %get-tuple-element.36), channel_id=1, source_target_pairs={{0,4},{4,8},{8,12},{1,5},{5,9},{9,13},{2,6},{6,10},{10,14},{3,7},{... | collective-permute-start | bytes 786440 | tf_op jit(solution)/shard_map/ppermute | solution.py:27
  190.7 11.1 %collective-permute-start.17 = (f32[2,8,8,512]{3,2,1,0:T(8,128)S(1)}, f32[2,8,8,512]{3,2,1,0:T(8,128)S(1)}, u32[]{:S(2)}, u32[]{:S(2)}) collective-permute-start(f32[2,8,8,512]{3,2,1,0:T(8,128)S(1)} %get-tuple-element.37), channel_id=1, source_target_pairs={{4,0},{8,4},{12,8},{5,1},{9,5},{13,9},{6,2},{10,6},{14,10},{7,3},{... | collective-permute-start | bytes 786440 | tf_op jit(solution)/shard_map/ppermute | solution.py:29
  202.0 3.0 %collective-permute-start.18 = (f32[2,5,32,512]{3,2,1,0:T(8,128)S(1)}, f32[2,5,32,512]{3,2,1,0:T(8,128)S(1)}, u32[]{:S(2)}, u32[]{:S(2)}) collective-permute-start(f32[2,5,32,512]{3,2,1,0:T(8,128)S(1)} %get-tuple-element.30), channel_id=1, source_target_pairs={{0,16},{1,17},{2,18},{3,19},{4,20},{5,21},{6,22},{7,23},{8,24},{9,... | collective-permute-start | bytes 1966088 | tf_op jit(solution)/shard_map/ppermute | solution.py:27
  203.4 4.0 %collective-permute-start.19 = (f32[2,5,32,512]{3,2,1,0:T(8,128)S(1)}, f32[2,5,32,512]{3,2,1,0:T(8,128)S(1)}, u32[]{:S(2)}, u32[]{:S(2)}) collective-permute-start(f32[2,5,32,512]{3,2,1,0:T(8,128)S(1)} %get-tuple-element.31), channel_id=1, source_target_pairs={{16,0},{17,1},{18,2},{19,3},{20,4},{21,5},{22,6},{23,7},{24,8},{25... | collective-permute-start | bytes 1966088 | tf_op jit(solution)/shard_map/ppermute | solution.py:29
